TPU v7x, 16 devices: a whole 2x2x2 slice. The times are simulated.
16 devices in a mesh: col: 4 (over z, y), row: 4 (over x, core).
Axes of the slice: x: 2, y: 2, z: 2, core: 2. Of those that a mesh axis runs over, the one named last changes fastest.
Arguments:
- vel_u: float32 [31, 128, 2048], P(None, 'row', 'col')
- vel_v: float32 [31, 128, 2048], P(None, 'row', 'col')
- temperature: float32 [31, 128, 2048], P(None, 'row', 'col')
- salinity: float32 [31, 128, 2048], P(None, 'row', 'col')
- surf_eta: float32 [128, 2048], P('row', 'col')
- trans_u: float32 [128, 2048], P('row', 'col')
- trans_v: float32 [128, 2048], P('row', 'col')
- bottom_depth: float32 [128, 2048], P('row', 'col')
- level_count: int32 [128, 2048], P('row', 'col')
- avg_weights: float32 [30], replicated
Outputs:
- output 1: float32 [128, 2048], P('row', 'col')
- output 2: float32 [128, 2048], P('row', 'col')
- output 3: float32 [128, 2048], P('row', 'col')
- output 4: float32 [31, 128, 2048], P(None, 'row', 'col')
- output 5: float32 [31, 128, 2048], P(None, 'row', 'col')
- output 6: float32 [31, 128, 2048], P(None, 'row', 'col')
- output 7: float32 [31, 128, 2048], P(None, 'row', 'col')
All inputs are finite; a program needn't handle non-finite values.
Results may differ from a plain program's by a relative error of at most 0.001.
Values sent between devices are 32-bit elements.
A program may use at most 1 GiB of HBM per device.

v0:
```python
import jax
import jax.numpy as jnp
from jax import lax
from jax.sharding import PartitionSpec as P

TIME_STEP = 1.0
GRAVITY = 16.0
BC_GRAVITY = 4.0
EXPAND_T = 0.2
CONTRACT_S = 0.6
CORIO_F0 = 0.4
CORIO_BETA = 0.4
VISC_R = 2.0
DIFF_R = 0.5


def shifted(padded, step_y, step_x):
    n_rows = padded.shape[-2] - 2
    n_cols = padded.shape[-1] - 2
    return padded[..., 1 + step_y:1 + step_y + n_rows, 1 + step_x:1 + step_x + n_cols]


def tri_solve(right_side, active, strength):
    link = strength * active[1:]
    zero_row = jnp.zeros_like(right_side[:1])
    low_links = jnp.concatenate([zero_row, link], axis=0)
    up_links = jnp.concatenate([link, zero_row], axis=0)

    def down(carry, level):
        ratio_prev, value_prev = carry
        low_link, up_link, target = level
        denominator = 1.0 + low_link + up_link + low_link * ratio_prev
        ratio = -up_link / denominator
        value = (target + low_link * value_prev) / denominator
        return (ratio, value), (ratio, value)

    start = (jnp.zeros_like(right_side[0]), jnp.zeros_like(right_side[0]))
    _, (ratios, values) = lax.scan(down, start, (low_links, up_links, right_side))

    def back(below, level):
        ratio, value = level
        solved = value - ratio * below
        return solved, solved

    _, solved_all = lax.scan(back, jnp.zeros_like(right_side[0]), (ratios, values), reverse=True)
    return solved_all


def ocean_columns(u_pad, v_pad, array_b15, salinity_pad, count_pad, depth_pad, coriolis_u, coriolis_v):
    n_levels = u_pad.shape[0]
    count_mid = shifted(count_pad, 0, 0)
    levels_u = jnp.minimum(count_mid, shifted(count_pad, 0, 1))
    levels_uw = jnp.minimum(shifted(count_pad, 0, -1), count_mid)
    levels_v = jnp.minimum(count_mid, shifted(count_pad, 1, 0))
    levels_vs = jnp.minimum(shifted(count_pad, -1, 0), count_mid)
    level_index = jnp.arange(n_levels)[:, None, None]
    mask_mid = (level_index < count_mid).astype(jnp.float32)
    mask_u = (level_index < levels_u).astype(jnp.float32)
    mask_uw = (level_index < levels_uw).astype(jnp.float32)
    mask_v = (level_index < levels_v).astype(jnp.float32)
    mask_vs = (level_index < levels_vs).astype(jnp.float32)
    u_mid = shifted(u_pad, 0, 0)
    v_mid = shifted(v_pad, 0, 0)
    u_west = shifted(u_pad, 0, -1)
    v_south = shifted(v_pad, -1, 0)
    v_at_u = 0.25 * (v_mid + shifted(v_pad, 0, 1) + v_south + shifted(v_pad, -1, 1))
    u_at_v = 0.25 * (u_mid + u_west + shifted(u_pad, 1, 0) + shifted(u_pad, 1, -1))
    inertia_u = 0.5 * (u_mid * (shifted(u_pad, 0, 1) - u_west) + v_at_u * (shifted(u_pad, 1, 0) - shifted(u_pad, -1, 0)))
    inertia_v = 0.5 * (u_at_v * (shifted(v_pad, 0, 1) - shifted(v_pad, 0, -1)) + v_mid * (shifted(v_pad, 1, 0) - v_south))
    density = CONTRACT_S * salinity_pad - EXPAND_T * array_b15
    pressure = (BC_GRAVITY / n_levels) * (jnp.cumsum(density, axis=0) - 0.5 * density)
    pressure_mid = shifted(pressure, 0, 0)
    u_star = u_mid + TIME_STEP * (coriolis_u * v_at_u - inertia_u - shifted(pressure, 0, 1) + pressure_mid)
    v_star = v_mid + TIME_STEP * (-coriolis_v * u_at_v - inertia_v - shifted(pressure, 1, 0) + pressure_mid)
    u_visc = tri_solve(u_star, mask_u, VISC_R)
    v_visc = tri_solve(v_star, mask_v, VISC_R)
    count_u = jnp.maximum(jnp.sum(mask_u, axis=0), 1.0)
    count_v = jnp.maximum(jnp.sum(mask_v, axis=0), 1.0)
    depth_mid = shifted(depth_pad, 0, 0)
    depth_u = 0.5 * (depth_mid + shifted(depth_pad, 0, 1))
    depth_v = 0.5 * (depth_mid + shifted(depth_pad, 1, 0))
    force_u = depth_u * jnp.sum(mask_u * (u_visc - u_mid), axis=0) / count_u / TIME_STEP
    force_v = depth_v * jnp.sum(mask_v * (v_visc - v_mid), axis=0) / count_v / TIME_STEP
    shear_u = u_visc - jnp.sum(mask_u * u_visc, axis=0) / count_u
    shear_v = v_visc - jnp.sum(mask_v * v_visc, axis=0) / count_v
    wet_u = (levels_u > 0).astype(jnp.float32)
    wet_v = (levels_v > 0).astype(jnp.float32)

    def advect(tracer_pad):
        tracer_mid = shifted(tracer_pad, 0, 0)
        flux_east = mask_u * u_mid * (tracer_mid + shifted(tracer_pad, 0, 1))
        flux_west = mask_uw * u_west * (shifted(tracer_pad, 0, -1) + tracer_mid)
        flux_north = mask_v * v_mid * (tracer_mid + shifted(tracer_pad, 1, 0))
        flux_south = mask_vs * v_south * (shifted(tracer_pad, -1, 0) + tracer_mid)
        return tracer_mid - 0.5 * TIME_STEP * (flux_east - flux_west + flux_north - flux_south)

    value_a15 = tri_solve(advect(array_b15), mask_mid, DIFF_R)
    salinity_new = tri_solve(advect(salinity_pad), mask_mid, DIFF_R)
    return (shear_u, shear_v, mask_u, mask_v, depth_u, depth_v, wet_u, wet_v, force_u, force_v, value_a15, salinity_new)


def fast_update(stack_pad, force_u, force_v, depth_u, depth_v, wet_u, wet_v, coriolis_u, coriolis_v, dt_fast):
    eta_pad = stack_pad[0]
    trans_u_pad = stack_pad[1]
    trans_v_pad = stack_pad[2]
    eta_ext = eta_pad[1:, 1:] - dt_fast * (trans_u_pad[1:, 1:] - trans_u_pad[1:, :-1] + trans_v_pad[1:, 1:] - trans_v_pad[:-1, 1:])
    eta_new = eta_ext[:-1, :-1]
    trans_u_old = shifted(trans_u_pad, 0, 0)
    trans_v_old = shifted(trans_v_pad, 0, 0)
    v_at_u = 0.25 * (trans_v_old + shifted(trans_v_pad, 0, 1) + shifted(trans_v_pad, -1, 0) + shifted(trans_v_pad, -1, 1))
    u_at_v = 0.25 * (trans_u_old + shifted(trans_u_pad, 0, -1) + shifted(trans_u_pad, 1, 0) + shifted(trans_u_pad, 1, -1))
    trans_u_new = wet_u * (trans_u_old + dt_fast * (coriolis_u * v_at_u + force_u - GRAVITY * depth_u * (eta_ext[:-1, 1:] - eta_new)))
    trans_v_new = wet_v * (trans_v_old + dt_fast * (force_v - coriolis_v * u_at_v - GRAVITY * depth_v * (eta_ext[1:, :-1] - eta_new)))
    return eta_new, trans_u_new, trans_v_new


def solution(mesh):
    n_col = mesh.shape['col']
    n_row = mesh.shape['row']
    east_moves = [(index, (index + 1) % n_col) for index in range(n_col)]
    west_moves = [(index, (index - 1) % n_col) for index in range(n_col)]
    north_moves = [(index, index + 1) for index in range(n_row - 1)]
    south_moves = [(index + 1, index) for index in range(n_row - 1)]

    def exchange(field):
        from_west = lax.ppermute(field[..., -1:], 'col', east_moves)
        from_east = lax.ppermute(field[..., :1], 'col', west_moves)
        wide = jnp.concatenate([from_west, field, from_east], axis=-1)
        from_south = lax.ppermute(wide[..., -1:, :], 'row', north_moves)
        from_north = lax.ppermute(wide[..., :1, :], 'row', south_moves)
        return jnp.concatenate([from_south, wide, from_north], axis=-2)

    def step(vel_u, vel_v, value_a11, salinity, surf_eta, trans_u, trans_v, bottom_depth, level_count, avg_weights):
        n_rows = surf_eta.shape[0]
        total_rows = n_rows * n_row
        dt_fast = TIME_STEP / avg_weights.shape[0]
        row_pos = (lax.axis_index('row') * n_rows + jnp.arange(n_rows)).astype(jnp.float32)[:, None]
        coriolis_u = CORIO_F0 + CORIO_BETA * ((row_pos + 0.5) / total_rows - 0.5)
        coriolis_v = CORIO_F0 + CORIO_BETA * ((row_pos + 1.0) / total_rows - 0.5)
        columns = ocean_columns(exchange(vel_u), exchange(vel_v), exchange(value_a11), exchange(salinity), exchange(level_count), exchange(bottom_depth), coriolis_u, coriolis_v)
        shear_u, shear_v, mask_u, mask_v, depth_u, depth_v, wet_u, wet_v, force_u, force_v, value_a15, salinity_new = columns

        def subcycle(carry, weight):
            eta_old, trans_u_old, trans_v_old, acc_u, acc_v = carry
            stack_pad = exchange(jnp.stack([eta_old, trans_u_old, trans_v_old]))
            eta_new, trans_u_new, trans_v_new = fast_update(stack_pad, force_u, force_v, depth_u, depth_v, wet_u, wet_v, coriolis_u, coriolis_v, dt_fast)
            return (eta_new, trans_u_new, trans_v_new, acc_u + weight * trans_u_new, acc_v + weight * trans_v_new), None

        zero_field = jnp.zeros_like(surf_eta)
        final, _ = lax.scan(subcycle, (surf_eta, trans_u, trans_v, zero_field, zero_field), avg_weights)
        eta_fin, trans_u_fin, trans_v_fin, bar_u, bar_v = final
        vel_u_new = mask_u * (shear_u + bar_u / depth_u)
        vel_v_new = mask_v * (shear_v + bar_v / depth_v)
        return (eta_fin, trans_u_fin, trans_v_fin, vel_u_new, vel_v_new, value_a15, salinity_new)

    cube = P(None, 'row', 'col')
    flat = P('row', 'col')
    return jax.shard_map(step, mesh=mesh, in_specs=(cube, cube, cube, cube, flat, flat, flat, flat, flat, P()), out_specs=(flat, flat, flat, cube, cube, cube, cube), check_vma=False)
```

profile of v0, /device:TPU:1, one launch (start us, length us, event | category | flops | bytes accessed | tf_op | source)
XLA Modules:
  0.0 1051.3 jit_solution(4368504904513202943)
XLA Ops:
  20.2 21.8 %collective-permute-done.21 = f32[32,1]{1,0:T(8,128)S(1)} collective-permute-done((f32[32,1]{1,0:T(8,128)S(1)}, f32[32,1]{1,0:T(8,128)S(1)}, u32[]{:S(2)}, u32[]{:S(2)}) %collective-permute-start.21) | collective-permute-done | bytes 160 | tf_op jit(solution)/shard_map/ppermute | solution.py:126
  70.3 18.9 %collective-permute-done.17 = f32[31,32,1]{2,1,0:T(8,128)S(1)} collective-permute-done((f32[31,32,1]{2,1,0:T(8,128)S(1)}, f32[31,32,1]{2,1,0:T(8,128)S(1)}, u32[]{:S(2)}, u32[]{:S(2)}) %collective-permute-start.17) | collective-permute-done | bytes 4000 | tf_op jit(solution)/shard_map/ppermute | solution.py:126
  92.7 7.7 collective-permute-done.18
  121.5 5.7 fusion.47
  130.3 52.6 %while.163 = (s32[]{:T(128)}, f32[32,512]{1,0:T(8,128)}, f32[32,512]{1,0:T(8,128)}, f32[31,32,512]{2,1,0:T(8,128)}, f32[31,32,512]{2,1,0:T(8,128)}, /*index=5*/f...) while((s32[]{:T(128)}, f32[32,512]{1,0:T(8,128)}, ...), condition=%wide.region_22.23_spmd.clone, body=%wide.region_21.22_spmd.clone.sunk | while | flops 180227 | bytes 590447 | solution.py:38
  184.4 48.6 %while.164 = (s32[]{:T(128)}, f32[32,512]{1,0:T(8,128)}, f32[31,32,512]{2,1,0:T(8,128)}, f32[31,32,512]{2,1,0:T(8,128)}, f32[31,32,512]{2,1,0:T(8,128)}, /*index=5*/s32[]{:T(128)}, s32[]{:T(128)}, s32[]{:T(128)}) while((s32[]{:T(128)}, f32[32,512]{1,0:T(8,128)}, f32[31,32,512]{2,1,0:T(8,128)}, f32[31,32,512]{2,1,0:T(8,128)}, ...), condition=%wide.region_24.25_spmd.clone, body=%wide.region_23.24_spmd.clone.sunk | while | flops 49156 | bytes 327791 | solution.py:45
  238.6 12.0 %fusion.60 = f32[31,32,512]{2,1,0:T(8,128)} fusion(f32[31,32,512]{2,1,0:T(8,128)} %param.30, f32[31,1,514]{2,1,0:T(1,128)} %collective-permute-done.19, f32[31,32,1]{2,1,0:T(8,128)} %copy-done.18, f32[31,32,1]{2,1,0:T(8,128)} %copy-done.17, f32[31,1,514]{2,1,0:T(1,128)} %collective-permute-done.20, f32[31,32,512]{2,1,0:T(8,128)S(1)} %copy-done, ...), kind=kLoop, calls=%fused_computation.136 | loop fusion | flops 15237120 | bytes 10559600 | tf_op jit(solution)/shard_map/sub | solution.py:95
  253.8 52.6 %while.161 = (s32[]{:T(128)}, f32[32,512]{1,0:T(8,128)}, f32[32,512]{1,0:T(8,128)}, f32[31,32,512]{2,1,0:T(8,128)}, f32[31,32,512]{2,1,0:T(8,128)}, /*index=5*/f...) while((s32[]{:T(128)}, f32[32,512]{1,0:T(8,128)}, ...), condition=%wide.region_18.19_spmd.clone, body=%wide.region_17.18_spmd.clone.sunk | while | flops 180227 | bytes 590447 | solution.py:38
  307.9 48.6 %while.162 = (s32[]{:T(128)}, f32[32,512]{1,0:T(8,128)}, f32[31,32,512]{2,1,0:T(8,128)}, f32[31,32,512]{2,1,0:T(8,128)}, f32[31,32,512]{2,1,0:T(8,128)}, /*index=5*/s32[]{:T(128)}, s32[]{:T(128)}, s32[]{:T(128)}) while((s32[]{:T(128)}, f32[32,512]{1,0:T(8,128)}, f32[31,32,512]{2,1,0:T(8,128)}, f32[31,32,512]{2,1,0:T(8,128)}, ...), condition=%wide.region_20.21_spmd.clone, body=%wide.region_19.20_spmd.clone.sunk | while | flops 49156 | bytes 327791 | solution.py:45
  356.6 10.9 %subtract_multiply_fusion = f32[31,34,514]{2,1,0:T(8,128)} fusion(f32[31,1,514]{2,1,0:T(1,128)} %collective-permute-done.20, f32[31,32,1]{2,1,0:T(8,128)} %copy-done.18, f32[31,32,512]{2,1,0:T(8,128)} %param.30, f32[31,32,1]{2,1,0:T(8,128)} %copy-done.17, f32[31,1,514]{2,1,0:T(1,128)} %collective-permute-done.19, f32[31,1,514]{2,1,0:T(1,128)} %copy-done.38, ...), kind=kOutput, calls=%fused_computation.109 | output fusion | flops 29796580 | bytes 6501072 | tf_op jit(solution)/shard_map/jit(cumsum)/reduce_window_sum | solution.py:71
  370.2 9.9 fusion.79
  383.2 49.6 %while.157 = (s32[]{:T(128)}, f32[32,512]{1,0:T(8,128)S(1)}, f32[32,512]{1,0:T(8,128)S(1)}, f32[31,32,512]{2,1,0:T(8,128)}, f32[31,32,512]{2,1,0:T(8,128)}, /*in...) while((s32[]{:T(128)}, f32[32,512]{1,0:T(8,128)S(1)}, ...), condition=%wide.region_2.3_spmd.clone, body=%wide.region_1.2_spmd.clone.sunk | while | flops 180227 | bytes 590447 | solution.py:38
  434.4 47.6 %while.158 = (s32[]{:T(128)}, f32[32,512]{1,0:T(8,128)S(1)}, f32[31,32,512]{2,1,0:T(8,128)}, f32[31,32,512]{2,1,0:T(8,128)}, f32[31,32,512]{2,1,0:T(8,128)}, /*index=5*/s32[]{:T(128)}, s32[]{:T(128)}, s32[]{:T(128)}) while((s32[]{:T(128)}, f32[32,512]{1,0:T(8,128)S(1)}, f32[31,32,512]{2,1,0:T(8,128)}, f32[31,32,512]{2,1,0:T(8,128)}, ...), condition=%wide.region_4.5_spmd.clone, body=%wide.region_3.4_spmd.clone.sunk | while | flops 49156 | bytes 327791 | solution.py:45
  484.3 10.5 fusion.70
  497.8 49.6 %while.159 = (s32[]{:T(128)}, f32[32,512]{1,0:T(8,128)S(1)}, f32[32,512]{1,0:T(8,128)S(1)}, f32[31,32,512]{2,1,0:T(8,128)}, f32[31,32,512]{2,1,0:T(8,128)}, /*in...) while((s32[]{:T(128)}, f32[32,512]{1,0:T(8,128)S(1)}, ...), condition=%wide.region_8.9_spmd.clone, body=%wide.region_7.8_spmd.clone.sunk | while | flops 180227 | bytes 590447 | solution.py:38
  549.0 47.9 %while.160 = (s32[]{:T(128)}, f32[32,512]{1,0:T(8,128)S(1)}, f32[31,32,512]{2,1,0:T(8,128)}, f32[31,32,512]{2,1,0:T(8,128)}, f32[31,32,512]{2,1,0:T(8,128)}, /*index=5*/s32[]{:T(128)}, s32[]{:T(128)}, s32[]{:T(128)}) while((s32[]{:T(128)}, f32[32,512]{1,0:T(8,128)S(1)}, f32[31,32,512]{2,1,0:T(8,128)}, f32[31,32,512]{2,1,0:T(8,128)}, ...), condition=%wide.region_10.11_spmd.clone, body=%wide.region_9.10_spmd.clone.sunk | while | flops 49156 | bytes 327791 | solution.py:45
  600.1 446.6 %while.165 = (s32[]{:T(128)}, f32[32,512]{1,0:T(8,128)S(1)}, f32[32,512]{1,0:T(8,128)S(1)}, f32[32,512]{1,0:T(8,128)S(1)}, f32[32,512]{1,0:T(8,128)S(1)}, /*inde...) while((s32[]{:T(128)}, f32[32,512]{1,0:T(8,128)S(1)}, ...), condition=%wide.region_14.15_spmd.clone.clone.clone, body=%wide.region_13.14_spmd.clone.clone.clone.sunk | while | flops 903904 | bytes 3474976 | solution.py:150
  637.0 5.6 collective-permute-start.3
  666.2 5.6 collective-permute-start.3
  696.6 5.6 collective-permute-start.3
  725.8 5.6 collective-permute-start.3
  756.1 5.6 collective-permute-start.3
  815.7 5.6 collective-permute-start.3
  964.0 5.6 collective-permute-start.3
  (952 shorter events, 910.7 us)
Async XLA Ops:
  1.5 16.3 %collective-permute-start.23 = (s32[32,1]{1,0:T(8,128)S(1)}, s32[32,1]{1,0:T(8,128)S(1)}, u32[]{:S(2)}, u32[]{:S(2)}) collective-permute-start(s32[32,1]{1,0:T(8,128)S(1)} %get-tuple-element.1216), channel_id=1, source_target_pairs={{0,4},{4,8},{8,12},{12,0},{1,5},{5,9},{9,13},{13,1},{2,6},{6,10},{... | collective-permute-start | bytes 392 | tf_op jit(solution)/shard_map/ppermute | solution.py:126
  3.6 15.4 %collective-permute-start.5 = (s32[32,1]{1,0:T(8,128)S(1)}, s32[32,1]{1,0:T(8,128)S(1)}, u32[]{:S(2)}, u32[]{:S(2)}) collective-permute-start(s32[32,1]{1,0:T(8,128)S(1)} %get-tuple-element.1217), channel_id=1, source_target_pairs={{0,12},{4,0},{8,4},{12,8},{1,13},{5,1},{9,5},{13,9},{2,14},{6,2},{... | collective-permute-start | bytes 392 | tf_op jit(solution)/shard_map/ppermute | solution.py:127
  6.9 51.5 %collective-permute-start.6 = (f32[31,32,1]{2,1,0:T(8,128)}, f32[31,32,1]{2,1,0:T(8,128)}, u32[]{:S(2)}, u32[]{:S(2)}) collective-permute-start(f32[31,32,1]{2,1,0:T(8,128)} %get-tuple-element.1191), channel_id=1, source_target_pairs={{0,12},{4,0},{8,4},{12,8},{1,13},{5,1},{9,5},{13,9},{2,14},{6,2},{... | collective-permute-start | bytes 11912 | tf_op jit(solution)/shard_map/ppermute | solution.py:127
  8.3 51.2 %collective-permute-start.7 = (f32[31,32,1]{2,1,0:T(8,128)}, f32[31,32,1]{2,1,0:T(8,128)}, u32[]{:S(2)}, u32[]{:S(2)}) collective-permute-start(f32[31,32,1]{2,1,0:T(8,128)} %get-tuple-element.1190), channel_id=1, source_target_pairs={{0,4},{4,8},{8,12},{12,0},{1,5},{5,9},{9,13},{13,1},{2,6},{6,10},{... | collective-permute-start | bytes 11912 | tf_op jit(solution)/shard_map/ppermute | solution.py:126
  16.4 46.5 %collective-permute-start.13 = (f32[31,32,1]{2,1,0:T(8,128)S(1)}, f32[31,32,1]{2,1,0:T(8,128)S(1)}, u32[]{:S(2)}, u32[]{:S(2)}) collective-permute-start(f32[31,32,1]{2,1,0:T(8,128)S(1)} %get-tuple-element.1196), channel_id=1, source_target_pairs={{0,4},{4,8},{8,12},{12,0},{1,5},{5,9},{9,13},{13,1},{2,6},{6,10},{... | collective-permute-start | bytes 11912 | tf_op jit(solution)/shard_map/ppermute | solution.py:126
  17.8 24.3 %collective-permute-start.21 = (f32[32,1]{1,0:T(8,128)S(1)}, f32[32,1]{1,0:T(8,128)S(1)}, u32[]{:S(2)}, u32[]{:S(2)}) collective-permute-start(f32[32,1]{1,0:T(8,128)S(1)} %get-tuple-element.1214), channel_id=1, source_target_pairs={{0,4},{4,8},{8,12},{12,0},{1,5},{5,9},{9,13},{13,1},{2,6},{6,10},{... | collective-permute-start | bytes 392 | tf_op jit(solution)/shard_map/ppermute | solution.py:126
  19.1 27.2 %collective-permute-start.4 = (f32[32,1]{1,0:T(8,128)S(1)}, f32[32,1]{1,0:T(8,128)S(1)}, u32[]{:S(2)}, u32[]{:S(2)}) collective-permute-start(f32[32,1]{1,0:T(8,128)S(1)} %get-tuple-element.1215), channel_id=1, source_target_pairs={{0,12},{4,0},{8,4},{12,8},{1,13},{5,1},{9,5},{13,9},{2,14},{6,2},{... | collective-permute-start | bytes 392 | tf_op jit(solution)/shard_map/ppermute | solution.py:127
  54.2 13.6 %collective-permute-start.14 = (f32[31,32,1]{2,1,0:T(8,128)S(1)}, f32[31,32,1]{2,1,0:T(8,128)S(1)}, u32[]{:S(2)}, u32[]{:S(2)}) collective-permute-start(f32[31,32,1]{2,1,0:T(8,128)S(1)} %get-tuple-element.1197), channel_id=1, source_target_pairs={{0,12},{4,0},{8,4},{12,8},{1,13},{5,1},{9,5},{13,9},{2,14},{6,2},{... | collective-permute-start | bytes 11912 | tf_op jit(solution)/shard_map/ppermute | solution.py:127
  57.1 47.8 %collective-permute-start.10 = (f32[31,32,1]{2,1,0:T(8,128)S(1)}, f32[31,32,1]{2,1,0:T(8,128)S(1)}, u32[]{:S(2)}, u32[]{:S(2)}) collective-permute-start(f32[31,32,1]{2,1,0:T(8,128)S(1)} %get-tuple-element.1192), channel_id=1, source_target_pairs={{0,4},{4,8},{8,12},{12,0},{1,5},{5,9},{9,13},{13,1},{2,6},{6,10},{... | collective-permute-start | bytes 11912 | tf_op jit(solution)/shard_map/ppermute | solution.py:126
  58.3 30.8 %collective-permute-start.17 = (f32[31,32,1]{2,1,0:T(8,128)S(1)}, f32[31,32,1]{2,1,0:T(8,128)S(1)}, u32[]{:S(2)}, u32[]{:S(2)}) collective-permute-start(f32[31,32,1]{2,1,0:T(8,128)S(1)} %get-tuple-element.1194), channel_id=1, source_target_pairs={{0,4},{4,8},{8,12},{12,0},{1,5},{5,9},{9,13},{13,1},{2,6},{6,10},{... | collective-permute-start | bytes 11912 | tf_op jit(solution)/shard_map/ppermute | solution.py:126
  61.7 38.7 %collective-permute-start.18 = (f32[31,32,1]{2,1,0:T(8,128)S(1)}, f32[31,32,1]{2,1,0:T(8,128)S(1)}, u32[]{:S(2)}, u32[]{:S(2)}) collective-permute-start(f32[31,32,1]{2,1,0:T(8,128)S(1)} %get-tuple-element.1195), channel_id=1, source_target_pairs={{0,12},{4,0},{8,4},{12,8},{1,13},{5,1},{9,5},{13,9},{2,14},{6,2},{... | collective-permute-start | bytes 11912 | tf_op jit(solution)/shard_map/ppermute | solution.py:127
  62.9 48.1 %collective-permute-start.9 = (f32[31,32,1]{2,1,0:T(8,128)S(1)}, f32[31,32,1]{2,1,0:T(8,128)S(1)}, u32[]{:S(2)}, u32[]{:S(2)}) collective-permute-start(f32[31,32,1]{2,1,0:T(8,128)S(1)} %get-tuple-element.1193), channel_id=1, source_target_pairs={{0,12},{4,0},{8,4},{12,8},{1,13},{5,1},{9,5},{13,9},{2,14},{6,2},{... | collective-permute-start | bytes 11912 | tf_op jit(solution)/shard_map/ppermute | solution.py:127
  68.2 531.0 %collective-permute-start.22 = (f32[1,514]{1,0:T(1,128)}, f32[1,514]{1,0:T(1,128)}, u32[]{:S(2)}, u32[]{:S(2)}) collective-permute-start(f32[1,514]{1,0:T(1,128)} %pad_maximum_fusion.52), channel_id=1, source_target_pairs={{1,0},{2,1},{3,2},{5,4},{6,5},{7,6},{9,8},{10,9},{11,10},{13,12},{... | collective-permute-start | bytes 6176 | tf_op jit(solution)/shard_map/ppermute | solution.py:130
  89.1 25.0 %collective-permute-start.8 = (f32[31,1,514]{2,1,0:T(1,128)S(1)}, f32[31,1,514]{2,1,0:T(1,128)S(1)}, u32[]{:S(2)}, u32[]{:S(2)}) collective-permute-start(f32[31,1,514]{2,1,0:T(1,128)S(1)} %get-tuple-element.1183), channel_id=1, source_target_pairs={{0,1},{1,2},{2,3},{4,5},{5,6},{6,7},{8,9},{9,10},{10,11},{12,13},{... | collective-permute-start | bytes 191216 | tf_op jit(solution)/shard_map/ppermute | solution.py:129
  101.6 18.0 %collective-permute-start.15 = (f32[31,1,514]{2,1,0:T(1,128)S(1)}, f32[31,1,514]{2,1,0:T(1,128)S(1)}, u32[]{:S(2)}, u32[]{:S(2)}) collective-permute-start(f32[31,1,514]{2,1,0:T(1,128)S(1)} %get-tuple-element.1188), channel_id=1, source_target_pairs={{0,1},{1,2},{2,3},{4,5},{5,6},{6,7},{8,9},{9,10},{10,11},{12,13},{... | collective-permute-start | bytes 191216 | tf_op jit(solution)/shard_map/ppermute | solution.py:129
  104.8 16.6 %collective-permute-start.16 = (f32[31,1,514]{2,1,0:T(1,128)S(1)}, f32[31,1,514]{2,1,0:T(1,128)S(1)}, u32[]{:S(2)}, u32[]{:S(2)}) collective-permute-start(f32[31,1,514]{2,1,0:T(1,128)S(1)} %get-tuple-element.1189), channel_id=1, source_target_pairs={{1,0},{2,1},{3,2},{5,4},{6,5},{7,6},{9,8},{10,9},{11,10},{13,12},{... | collective-permute-start | bytes 191216 | tf_op jit(solution)/shard_map/ppermute | solution.py:130
  112.2 124.5 %collective-permute-start.19 = (f32[31,1,514]{2,1,0:T(1,128)}, f32[31,1,514]{2,1,0:T(1,128)}, u32[]{:S(2)}, u32[]{:S(2)}) collective-permute-start(f32[31,1,514]{2,1,0:T(1,128)} %get-tuple-element.1186), channel_id=1, source_target_pairs={{0,1},{1,2},{2,3},{4,5},{5,6},{6,7},{8,9},{9,10},{10,11},{12,13},{... | collective-permute-start | bytes 191216 | tf_op jit(solution)/shard_map/ppermute | solution.py:129
  116.5 122.1 %collective-permute-start.20 = (f32[31,1,514]{2,1,0:T(1,128)}, f32[31,1,514]{2,1,0:T(1,128)}, u32[]{:S(2)}, u32[]{:S(2)}) collective-permute-start(f32[31,1,514]{2,1,0:T(1,128)} %get-tuple-element.1187), channel_id=1, source_target_pairs={{1,0},{2,1},{3,2},{5,4},{6,5},{7,6},{9,8},{10,9},{11,10},{13,12},{... | collective-permute-start | bytes 191216 | tf_op jit(solution)/shard_map/ppermute | solution.py:130
  119.5 248.0 %collective-permute-start.11 = (f32[31,1,514]{2,1,0:T(1,128)}, f32[31,1,514]{2,1,0:T(1,128)}, u32[]{:S(2)}, u32[]{:S(2)}) collective-permute-start(f32[31,1,514]{2,1,0:T(1,128)} %get-tuple-element.1184), channel_id=1, source_target_pairs={{1,0},{2,1},{3,2},{5,4},{6,5},{7,6},{9,8},{10,9},{11,10},{13,12},{... | collective-permute-start | bytes 191216 | tf_op jit(solution)/shard_map/ppermute | solution.py:130
  233.0 136.6 %collective-permute-start.12 = (f32[31,1,514]{2,1,0:T(1,128)}, f32[31,1,514]{2,1,0:T(1,128)}, u32[]{:S(2)}, u32[]{:S(2)}) collective-permute-start(f32[31,1,514]{2,1,0:T(1,128)} %get-tuple-element.1185), channel_id=1, source_target_pairs={{0,1},{1,2},{2,3},{4,5},{5,6},{6,7},{8,9},{9,10},{10,11},{12,13},{... | collective-permute-start | bytes 191216 | tf_op jit(solution)/shard_map/ppermute | solution.py:129
  236.7 247.5 %collective-permute-start.25 = (f32[31,1,514]{2,1,0:T(1,128)}, f32[31,1,514]{2,1,0:T(1,128)}, u32[]{:S(2)}, u32[]{:S(2)}) collective-permute-start(f32[31,1,514]{2,1,0:T(1,128)} %get-tuple-element.1182), channel_id=1, source_target_pairs={{1,0},{2,1},{3,2},{5,4},{6,5},{7,6},{9,8},{10,9},{11,10},{13,12},{... | collective-permute-start | bytes 191216 | tf_op jit(solution)/shard_map/ppermute | solution.py:130
  664.3 8.2 collective-permute-start.2
  694.6 8.2 collective-permute-start.2
  723.8 8.2 collective-permute-start.2
  (169 other events, 1790.0 us)
where the time goes:
time: 1070 us; the launch traced here: 1050 us
  other arithmetic  535 us (50%)
  starting transfers between devices  308 us (29%)
  waiting for transfers between devices  153 us (14%)
  local copies, waits for them, and re-layouts  51.3 us (5%)
    dynamic_update_slice x248, other arithmetic, tri_solve(): lax.scan(down, start, (low_links, up_links, right_side))  397 us
    ppermute x35, starting transfers between devices, exchange(): from_south = lax.ppermute(wide[..., -1:, :], 'row', north_moves)  179 us
    ppermute x36, waiting for transfers between devices, exchange(): from_west = lax.ppermute(field[..., -1:], 'col', east_moves)  87.3 us
    ppermute x36, starting transfers between devices, exchange(): from_north = lax.ppermute(wide[..., :1, :], 'row', south_moves)  72.7 us
    ppermute x36, waiting for transfers between devices, exchange(): from_east = lax.ppermute(field[..., :1], 'col', west_moves)  61.1 us
    ppermute x36, starting transfers between devices, exchange(): from_west = lax.ppermute(field[..., -1:], 'col', east_moves)  33.8 us
    add x30, other arithmetic, subcycle(): acc_u + weight * trans_u_new  25 us
    add x30, other arithmetic, subcycle(): acc_v + weight * trans_v_new  23.5 us
  transfers between devices with their start and end apart: 143, of which 95 were waited for; matrix products, arithmetic and copies ran while one was open for 49% of the time, Pallas kernels for 0%

commit v1 on v0

v1 whole, which is shorter than its diff:
```python
import functools

import jax
import jax.numpy as jnp
import numpy as np
from jax import lax
from jax.experimental import pallas as pl
from jax.experimental.pallas import tpu as pltpu
from jax.sharding import PartitionSpec as P

TIME_STEP = 1.0
GRAVITY = 16.0
BC_GRAVITY = 4.0
EXPAND_T = 0.2
CONTRACT_S = 0.6
CORIO_F0 = 0.4
CORIO_BETA = 0.4
VISC_R = 2.0
DIFF_R = 0.5

LEV = 31
SLOT = 32
NR = 32
NC = 512
NT = 4
L = 128
R0 = 8
PR = 48
XR = 112
XO = 40
MESH = pl.DeviceIdType.MESH
f32 = jnp.float32


def solve_table(n_levels):
    rows = []
    for s in (VISC_R, DIFF_R):
        scale, carry, link, last = np.zeros((4, SLOT))
        ratio = 0.0
        for k in range(n_levels):
            low = s if k else 0.0
            full = 1.0 + low + s - low * ratio
            end = 1.0 + low - low * ratio
            scale[k], carry[k], link[k], last[k] = 1.0 / full, low / full, s / full, full / end
            ratio = s / full
        rows += [scale, carry, link, last]
    return np.concatenate(rows).astype(np.float32)


def ocean_kernel(axes, n_col, n_row, n_sub, *refs):
    (u_h, v_h, t_h, s_h, eta_h, tu_h, tv_h, dep_h, cnt_h, w_s, tab_s,
     eta_o, tu_o, tv_o, gu_o, gv_o, cu_o, cv_o, cc_o, xu_o, xv_o, xt_o, xs_o,
     bu, bv, bt, bs, xu, xv, xt, xs, cnt_i, pc, pp, ce,
     pw, pe, rw, re, x, xf, qw, qe, we, ww, fw, fe, fre, frw,
     fu4, fv4, cu, cv, cvs, hu, hv, su, sv,
     ca, cb, cc, cd, cg, ch, cm, cn, tt, ss, au, av,
     lsem, ssem, rsem, osem) = refs
    col = lax.axis_index('col')
    row = lax.axis_index('row')
    east = lax.rem(col + 1, n_col)
    west = lax.rem(col + n_col - 1, n_col)
    has_s = row > 0
    has_n = row < n_row - 1

    def dev(c, r):
        at = {'col': c, 'row': r}
        return tuple(at[name] for name in axes)

    bufs = (bu, bv, bt, bs)
    loads = []
    for f, (src, dst) in enumerate(zip((u_h, v_h, t_h, s_h), bufs)):
        for t in range(NT):
            loads.append(pltpu.make_async_copy(src.at[:, :, L * t:L * t + L], dst.at[t, 0:LEV, R0:R0 + NR, :], lsem.at[len(loads)]))
    flat_loads = []
    for f, src in enumerate((eta_h, tu_h, tv_h)):
        for t in range(NT):
            flat_loads.append(pltpu.make_async_copy(src.at[:, L * t:L * t + L], x.at[f, t, XO:XO + NR, :], lsem.at[len(loads) + len(flat_loads)]))
    for t in range(NT):
        flat_loads.append(pltpu.make_async_copy(dep_h.at[:, L * t:L * t + L], bv.at[t, LEV, R0:R0 + NR, :], lsem.at[len(loads) + len(flat_loads)]))
    for t in range(NT):
        flat_loads.append(pltpu.make_async_copy(cnt_h.at[:, L * t:L * t + L], cnt_i.at[t], lsem.at[len(loads) + len(flat_loads)]))
    for cp in flat_loads + loads:
        cp.start()

    zero = functools.partial(jnp.zeros, dtype=f32)
    for f in range(4):
        for t in range(NT + 1):
            x[f, t, 0:8, :] = zero((8, L))
            x[f, t, XR - 8:XR, :] = zero((8, L))
    for t in range(NT + 1):
        tt[t, XR - 8:XR, :] = zero((8, L))
    for t in range(NT):
        bt[t, LEV, R0:R0 + NR, :] = zero((NR, L))
        bs[t, LEV, R0:R0 + NR, :] = zero((NR, L))
        for a in (xu, xv, xt, xs):
            a[t, 0] = zero((NR, L))

    @pl.when(jnp.logical_not(has_s))
    def _():
        for b in bufs:
            b[:, :, R0 - 8:R0, :] = zero((NT, SLOT, 8, L))
        re[R0 - 8:R0, :] = zero((8, L))
        x[:, 0:NT, 8:XO, :] = zero((4, NT, NR, L))
        xf[:, 0:NT, 8:XO, :] = zero((2, NT, NR, L))
        for a in (we, ww, fre, frw):
            a[0] = zero((NR, L))

    @pl.when(jnp.logical_not(has_n))
    def _():
        for b in bufs:
            b[:, :, R0 + NR:PR, :] = zero((NT, SLOT, 8, L))
        rw[R0 + NR:PR, :] = zero((8, L))
        x[:, 0:NT, XO + NR:XO + 2 * NR, :] = zero((4, NT, NR, L))
        xf[:, 0:NT, XO + NR:XO + 2 * NR, :] = zero((2, NT, NR, L))
        for a in (we, ww, fre, frw):
            a[2] = zero((NR, L))

    barrier = pltpu.get_barrier_semaphore()

    def signal(c, r):
        pl.semaphore_signal(barrier, inc=1, device_id=dev(c, r), device_id_type=MESH)

    signal(west, row)
    signal(east, row)

    @pl.when(has_s)
    def _():
        for c in (west, col, east):
            signal(c, row - 1)

    @pl.when(has_n)
    def _():
        for c in (west, col, east):
            signal(c, row + 1)

    edge = jnp.logical_or(row == 0, row == n_row - 1)

    @pl.when(edge)
    def _():
        pl.semaphore_wait(barrier, 5)

    @pl.when(jnp.logical_not(edge))
    def _():
        pl.semaphore_wait(barrier, 8)

    n_copies = 0

    def remote(src, dst, c, r, sends, receives):
        nonlocal n_copies
        i = n_copies
        n_copies += 1
        return (pltpu.make_async_remote_copy(src, dst, ssem.at[i], rsem.at[i], device_id=dev(c, r), device_id_type=MESH), sends, receives)

    def maybe(cond, fn):
        if cond is None:
            fn()
        else:
            pl.when(cond)(fn)

    def start(group):
        for cp, sends, _ in group:
            maybe(sends, cp.start)

    def arrive(group):
        for cp, _, receives in group:
            maybe(receives, cp.wait_recv)

    def drain(group):
        for cp, sends, _ in group:
            maybe(sends, cp.wait_send)

    def rows_of(b):
        return [remote(b.at[:, :, R0 + NR - 1:R0 + NR, :], b.at[:, :, R0 - 1:R0, :], col, row + 1, has_n, has_s),
                remote(b.at[:, :, R0:R0 + 1, :], b.at[:, :, R0 + NR:R0 + NR + 1, :], col, row - 1, has_s, has_n)]

    def wide_of(b, lanes_w, lanes_e, from_e, from_w):
        own = b.at[:, 0:NT, XO:XO + NR, :]
        return [remote(own, b.at[:, 0:NT, 8:XO, :], col, row + 1, has_n, has_s),
                remote(own, b.at[:, 0:NT, XO + NR:XO + 2 * NR, :], col, row - 1, has_s, has_n),
                remote(lanes_w, from_e.at[1], west, row, None, None),
                remote(lanes_e, from_w.at[1], east, row, None, None),
                remote(lanes_w, from_e.at[2], west, row - 1, has_s, has_n),
                remote(lanes_e, from_w.at[2], east, row - 1, has_s, has_n),
                remote(lanes_w, from_e.at[0], west, row + 1, has_n, has_s),
                remote(lanes_e, from_w.at[0], east, row + 1, has_n, has_s)]

    row_group = rows_of(bu) + rows_of(bv) + rows_of(bt) + rows_of(bs)
    lane_group = [remote(pw, re.at[R0:R0 + NR, :], west, row, None, None),
                  remote(pe, rw.at[R0:R0 + NR, :], east, row, None, None),
                  remote(pe.at[0:1, :], rw.at[R0 + NR:R0 + NR + 1, :], east, row - 1, has_s, has_n),
                  remote(pw.at[NR - 1:NR, :], re.at[R0 - 1:R0, :], west, row + 1, has_n, has_s)]
    wide_group = wide_of(x, qw, qe, we, ww)
    force_group = wide_of(xf, fw, fe, fre, frw)

    lane = lax.broadcasted_iota(jnp.int32, (NR, L), 1)

    for cp in flat_loads:
        cp.wait()
    for t in range(NT):
        count = cnt_i[t].astype(f32)
        bu[t, LEV, R0:R0 + NR, :] = count
        x[3, t, XO:XO + NR, :] = jnp.where(count > 0.0, bv[t, LEV, R0:R0 + NR, :], 0.0)

    def roll(a, shift):
        return pltpu.roll(a, shift, 1) if not (isinstance(shift, int) and shift % L == 0) else a

    def pack_wide(b, n_fields):
        first = last = zero((NR, L))
        for f in range(n_fields):
            mine = (lane >= 32 * f) & (lane < 32 * f + 32)
            first = jnp.where(mine, roll(b[f, 0, XO:XO + NR, :], 32 * f), first)
            last = jnp.where(mine, roll(b[f, NT - 1, XO:XO + NR, :], (32 * f + 32) % L), last)
        return first, last

    first, last = pack_wide(x, 4)
    qw[...] = first
    qe[...] = last

    for cp in loads:
        cp.wait()
    first = last = zero((NR, L))
    for f, b in enumerate(bufs):
        for k in range(SLOT):
            p = SLOT * f + k
            first = jnp.where(lane == p, roll(b[0, k, R0:R0 + NR, :], p), first)
            last = jnp.where(lane == p, roll(b[NT - 1, k, R0:R0 + NR, :], (p + 1) % L), last)
    pw[...] = first
    pe[...] = last
    start(row_group)
    start(lane_group)
    start(wide_group)

    row_pos = (row * NR + lax.broadcasted_iota(jnp.int32, (NR, L), 0)).astype(f32)
    total_rows = NR * n_row
    fu4[...] = 0.25 * (CORIO_F0 + CORIO_BETA * ((row_pos + 0.5) / total_rows - 0.5))
    fv4[...] = 0.25 * (CORIO_F0 + CORIO_BETA * ((row_pos + 1.0) / total_rows - 0.5))

    def to_east(tiles, halo):
        rolled = [roll(a, L - 1) for a in tiles] + [halo]
        return [jnp.where(lane == L - 1, rolled[t + 1], rolled[t]) for t in range(NT)]

    def to_west(tiles, halo):
        rolled = [halo] + [roll(a, 1) for a in tiles]
        return [jnp.where(lane == 0, rolled[t], rolled[t + 1]) for t in range(NT)]

    def east_lane(f, k, lo=R0):
        return pltpu.roll(re[lo:lo + NR, :], L - 1 - (SLOT * f + k), 1)

    def west_lane(f, k, lo=R0):
        return pltpu.roll(rw[lo:lo + NR, :], lax.rem(L - (SLOT * f + k), L), 1)

    arrive(row_group)
    arrive(lane_group)

    def level(b, k, lo=R0):
        return [b[t, k, lo:lo + NR, :] for t in range(NT)]

    c_mid, d_mid = level(bu, LEV), level(bv, LEV)
    c_east = to_east(c_mid, east_lane(0, LEV))
    d_east = to_east(d_mid, east_lane(1, LEV))
    c_north, c_south = level(bu, LEV, R0 + 1), level(bu, LEV, R0 - 1)
    d_north = level(bv, LEV, R0 + 1)
    for t in range(NT):
        cu[t] = jnp.minimum(c_mid[t], c_east[t])
        cv[t] = jnp.minimum(c_mid[t], c_north[t])
        cvs[t] = jnp.minimum(c_mid[t], c_south[t])
        hu[t] = 0.5 * (d_mid[t] + d_east[t])
        hv[t] = 0.5 * (d_mid[t] + d_north[t])
        cu_o[t] = jnp.minimum(c_mid[t], c_east[t])
        cv_o[t] = jnp.minimum(c_mid[t], c_north[t])
        cc_o[t] = c_mid[t]

    for t in range(NT):
        pc[t] = zero((NR + 8, L))
    ce[...] = zero((NR, L))
    p_scale = BC_GRAVITY / LEV

    def momentum_down(k, _):
        prev = jnp.maximum(k - 1, 0)
        scale, carry = tab_s[k], tab_s[SLOT + k]
        um, un, us = level(bu, k), level(bu, k, R0 + 1), level(bu, k, R0 - 1)
        vm, vn, vs = level(bv, k), level(bv, k, R0 + 1), level(bv, k, R0 - 1)
        ue = to_east(um, east_lane(0, k))
        uw = to_west(um, west_lane(0, k))
        unw = to_west(un, west_lane(0, k, R0 + 1))
        ve = to_east(vm, east_lane(1, k))
        vw = to_west(vm, west_lane(1, k))
        vse = to_east(vs, east_lane(1, k, R0 - 1))
        pm = []
        for t in range(NT):
            density = CONTRACT_S * bs[t, k, R0:PR, :] - EXPAND_T * bt[t, k, R0:PR, :]
            total = pc[t] + density
            pc[t] = total
            pressure = p_scale * (total - 0.5 * density)
            pp[t] = pressure
            pm.append(pressure[:NR])
        density = CONTRACT_S * east_lane(3, k) - EXPAND_T * east_lane(2, k)
        total = ce[...] + density
        ce[...] = total
        pe_ = to_east(pm, p_scale * (total - 0.5 * density))
        for t in range(NT):
            pn = pp[t, 1:NR + 1, :]
            vb4 = (vm[t] + ve[t]) + (vs[t] + vse[t])
            ub4 = (um[t] + uw[t]) + (un[t] + unw[t])
            u_star = um[t] + vb4 * (fu4[...] - 0.125 * (un[t] - us[t])) - um[t] * (0.5 * (ue[t] - uw[t])) + (pm[t] - pe_[t])
            v_star = vm[t] - ub4 * (fv4[...] + 0.125 * (ve[t] - vw[t])) - vm[t] * (0.5 * (vn[t] - vs[t])) + (pm[t] - pn)
            xu[t, k] = scale * u_star + carry * xu[t, prev]
            xv[t, k] = scale * v_star + carry * xv[t, prev]
        return 0

    lax.fori_loop(0, LEV, momentum_down, 0)

    for t in range(NT):
        def momentum_up(i, state, t=t):
            k = LEV - 1 - i
            link, last_ = tab_s[2 * SLOT + k], tab_s[3 * SLOT + k]
            kf = k.astype(f32)
            out = []
            for sweep, b, count, (below, sum_x, sum_0) in ((xu, bu, cu, state[:3]), (xv, bv, cv, state[3:])):
                value = sweep[t, k]
                active = count[t] > kf
                solved = jnp.where(count[t] > kf + 1.0, value + link * below, jnp.where(active, last_ * value, 0.0))
                sweep[t, k] = solved
                out += [solved, sum_x + solved, sum_0 + jnp.where(active, b[t, k, R0:R0 + NR, :], 0.0)]
            return tuple(out)

        z = zero((NR, L))
        _, ux, u0, _, vx, v0 = lax.fori_loop(0, LEV, momentum_up, (z,) * 6)
        for q, h, mean, count, total, start_ in ((0, hu, su, cu, ux, u0), (1, hv, sv, cv, vx, v0)):
            n_active = jnp.maximum(count[t], 1.0)
            mean[t] = total / n_active
            xf[q, t, XO:XO + NR, :] = h[t] * (total - start_) / n_active / TIME_STEP

    stores = [pltpu.make_async_copy(a, o, osem.at[i]) for i, (a, o) in enumerate(((xu, xu_o), (xv, xv_o), (xt, xt_o), (xs, xs_o)))]
    first, last = pack_wide(xf, 2)
    fw[...] = first
    fe[...] = last
    start(force_group)
    stores[0].start()
    stores[1].start()

    c_west0 = jnp.minimum(west_lane(0, LEV), bu[0, LEV, R0:R0 + NR, :])

    def tracer_down(k, _):
        prev = jnp.maximum(k - 1, 0)
        scale, carry = tab_s[4 * SLOT + k], tab_s[5 * SLOT + k]
        kf = k.astype(f32)
        um = [jnp.where(cu[t] > kf, bu[t, k, R0:R0 + NR, :], 0.0) for t in range(NT)]
        vm = [jnp.where(cv[t] > kf, bv[t, k, R0:R0 + NR, :], 0.0) for t in range(NT)]
        vs = [jnp.where(cvs[t] > kf, bv[t, k, R0 - 1:R0 - 1 + NR, :], 0.0) for t in range(NT)]
        uw0 = jnp.where(c_west0 > kf, west_lane(0, k), 0.0)
        for f, b, sweep in ((2, bt, xt), (3, bs, xs)):
            q = level(b, k)
            qe_ = to_east(q, east_lane(f, k))
            f_east = [um[t] * (q[t] + qe_[t]) for t in range(NT)]
            f_west = to_west(f_east, uw0 * (west_lane(f, k) + q[0]))
            for t in range(NT):
                f_north = vm[t] * (q[t] + b[t, k, R0 + 1:R0 + 1 + NR, :])
                f_south = vs[t] * (b[t, k, R0 - 1:R0 - 1 + NR, :] + q[t])
                new = q[t] - 0.5 * TIME_STEP * (f_east[t] - f_west[t] + f_north - f_south)
                sweep[t, k] = jnp.where(bu[t, LEV, R0:R0 + NR, :] > kf, scale * new + carry * sweep[t, prev], new)
        return 0

    lax.fori_loop(0, LEV, tracer_down, 0)
    stores[2].start()
    stores[3].start()

    arrive(wide_group)
    drain(wide_group)
    arrive(force_group)

    def unpack_wide(b, from_e, from_w, n_fields):
        for f in range(n_fields):
            for seg in range(3):
                b[f, NT, 8 + NR * seg:8 + NR * seg + NR, :] = jnp.where(lane < L // 2, roll(from_e[seg], (L - 32 * f) % L), roll(from_w[seg], (96 - 32 * f) % L))

    unpack_wide(x, we, ww, 4)
    unpack_wide(xf, fre, frw, 2)
    dt_fast = TIME_STEP / n_sub
    XT = NT + 1

    def ring_east(tiles, last_lane):
        rolled = [roll(a, L - 1) for a in tiles]
        return [jnp.where(last_lane, rolled[(t + 1) % XT], rolled[t]) for t in range(XT)]

    def ring_west(tiles, first_lane):
        rolled = [roll(a, 1) for a in tiles]
        return [jnp.where(first_lane, rolled[(t - 1) % XT], rolled[t]) for t in range(XT)]

    for seg in range(3):
        lo = 8 + NR * seg
        pos = (row * NR + NR * (seg - 1) + lax.broadcasted_iota(jnp.int32, (NR, L), 0)).astype(f32)
        f_u = CORIO_F0 + CORIO_BETA * ((pos + 0.5) / total_rows - 0.5)
        f_v = CORIO_F0 + CORIO_BETA * ((pos + 1.0) / total_rows - 0.5)
        d = [x[3, t, lo:lo + NR, :] for t in range(XT)]
        d_e = ring_east(d, lane == L - 1)
        for t in range(XT):
            d_n = x[3, t, lo + 1:lo + 1 + NR, :]
            wet = jnp.where((d[t] > 0.0) & (d_e[t] > 0.0), 1.0, 0.0)
            cm[t, lo:lo + NR, :] = wet
            ca[t, lo:lo + NR, :] = (0.25 * dt_fast) * f_u * wet
            cb[t, lo:lo + NR, :] = (dt_fast * GRAVITY * 0.5) * (d[t] + d_e[t]) * wet
            cc[t, lo:lo + NR, :] = dt_fast * xf[0, t, lo:lo + NR, :] * wet
            wet = jnp.where((d[t] > 0.0) & (d_n > 0.0), 1.0, 0.0)
            cn[t, lo:lo + NR, :] = wet
            cd[t, lo:lo + NR, :] = (0.25 * dt_fast) * f_v * wet
            cg[t, lo:lo + NR, :] = (dt_fast * GRAVITY * 0.5) * (d[t] + d_n) * wet
            ch[t, lo:lo + NR, :] = dt_fast * xf[1, t, lo:lo + NR, :] * wet

    for t in range(NT):
        au[t] = zero((NR, L))
        av[t] = zero((NR, L))

    def subcycle(lo, hi, chunk, n, _):
        lane_c = lax.broadcasted_iota(jnp.int32, (chunk, L), 1)
        first_lane, last_lane = lane_c == 0, lane_c == L - 1
        weight = w_s[n]
        for r in range(lo, hi, chunk):
            u_t = [x[1, t, r:r + chunk, :] for t in range(XT)]
            u_w = ring_west(u_t, first_lane)
            for t in range(XT):
                v_t, v_s = x[2, t, r:r + chunk, :], x[2, t, r - 1:r - 1 + chunk, :]
                x[0, t, r:r + chunk, :] = x[0, t, r:r + chunk, :] - dt_fast * ((u_t[t] - u_w[t]) + (v_t - v_s))
                tt[t, r:r + chunk, :] = u_t[t] + u_w[t]
                ss[t, r:r + chunk, :] = v_t + v_s
        for r in range(lo, hi, chunk):
            e_t = [x[0, t, r:r + chunk, :] for t in range(XT)]
            e_e = ring_east(e_t, last_lane)
            s_t = [ss[t, r:r + chunk, :] for t in range(XT)]
            s_e = ring_east(s_t, last_lane)
            for t in range(XT):
                at = (t, slice(r, r + chunk))
                up = (t, slice(r + 1, r + 1 + chunk))
                e_n = x[0, t, r + 1:r + 1 + chunk, :]
                x[1, t, r:r + chunk, :] = cm[at] * x[1, t, r:r + chunk, :] + ca[at] * (s_t[t] + s_e[t]) + cc[at] - cb[at] * (e_e[t] - e_t[t])
                x[2, t, r:r + chunk, :] = cn[at] * x[2, t, r:r + chunk, :] - cd[at] * (tt[at] + tt[up]) + ch[at] - cg[at] * (e_n - e_t[t])
        for t in range(NT):
            au[t] += weight * x[1, t, XO:XO + NR, :]
            av[t] += weight * x[2, t, XO:XO + NR, :]
        return 0

    done = 0
    for side in (4, 3, 2, 1):
        until = n_sub - 8 * (side - 1)
        rows = NR + 16 * side
        chunk = {4: 32, 3: 40, 2: 32, 1: 24}[side]
        lax.fori_loop(done, until, functools.partial(subcycle, XO - 8 * side, XO - 8 * side + rows, chunk), 0)
        done = until

    for t in range(NT):
        cols = slice(L * t, L * t + L)
        eta_o[:, cols] = x[0, t, XO:XO + NR, :]
        tu_o[:, cols] = x[1, t, XO:XO + NR, :]
        tv_o[:, cols] = x[2, t, XO:XO + NR, :]
        gu_o[t] = au[t] / hu[t] - su[t]
        gv_o[t] = av[t] / hv[t] - sv[t]

    for group in (row_group, lane_group, force_group):
        drain(group)
    for cp in stores:
        cp.wait()


def final_kernel(tab_s, xu, xv, xt, xs, gu, gv, cu, cv, cc, u_o, v_o, t_o, s_o):
    rows = u_o.shape[1]
    g_u, g_v, c_u, c_v, c_c = gu[0], gv[0], cu[0], cv[0], cc[0]

    def up(i, state):
        k = LEV - 1 - i
        kf = k.astype(f32)
        link, last = tab_s[6 * SLOT + k], tab_s[7 * SLOT + k]
        u_o[k] = jnp.where(c_u > kf, xu[0, k] + g_u, 0.0)
        v_o[k] = jnp.where(c_v > kf, xv[0, k] + g_v, 0.0)
        inner, active = c_c > kf + 1.0, c_c > kf
        out = []
        for sweep, o, below in ((xt, t_o, state[0]), (xs, s_o, state[1])):
            value = sweep[0, k]
            solved = jnp.where(inner, value + link * below, jnp.where(active, last * value, value))
            o[k] = solved
            out.append(solved)
        return tuple(out)

    z = jnp.zeros((rows, L), f32)
    lax.fori_loop(0, LEV, up, (z, z))


def solution(mesh):
    n_col = mesh.shape['col']
    n_row = mesh.shape['row']

    def step(vel_u, vel_v, value_a11, salinity, surf_eta, trans_u, trans_v, bottom_depth, level_count, avg_weights):
        n_sub = avg_weights.shape[0]
        table = jnp.asarray(solve_table(LEV))
        hbm = pl.BlockSpec(memory_space=pl.ANY)
        vmem = pl.BlockSpec(memory_space=pltpu.VMEM)
        smem = pl.BlockSpec(memory_space=pltpu.SMEM)
        flat = jax.ShapeDtypeStruct((NR, NC), f32)
        tile = jax.ShapeDtypeStruct((NT, NR, L), f32)
        sweep = jax.ShapeDtypeStruct((NT, SLOT, NR, L), f32)
        V = pltpu.VMEM
        wide = (NT + 1, XR, L)
        scratch = ([V((NT, SLOT, PR, L), f32)] * 4 + [V((NT, SLOT, NR, L), f32)] * 4
                   + [V((NT, NR, L), jnp.int32), V((NT, NR + 8, L), f32), V((NT, NR + 8, L), f32), V((NR, L), f32)]
                   + [V((NR, L), f32)] * 2 + [V((PR, L), f32)] * 2
                   + [V((4,) + wide, f32), V((2,) + wide, f32)] + [V((NR, L), f32)] * 2 + [V((3, NR, L), f32)] * 2
                   + [V((NR, L), f32)] * 2 + [V((3, NR, L), f32)] * 2
                   + [V((NR, L), f32)] * 2 + [V((NT, NR, L), f32)] * 7
                   + [V(wide, f32)] * 10 + [V((NT, NR, L), f32)] * 2
                   + [pltpu.SemaphoreType.DMA((40,)), pltpu.SemaphoreType.DMA((28,)), pltpu.SemaphoreType.DMA((28,)), pltpu.SemaphoreType.DMA((4,))])
        outs = pl.pallas_call(
            functools.partial(ocean_kernel, tuple(mesh.axis_names), n_col, n_row, n_sub),
            out_shape=[flat] * 3 + [tile] * 5 + [sweep] * 4,
            in_specs=[hbm] * 9 + [smem] * 2,
            out_specs=[vmem] * 8 + [hbm] * 4,
            scratch_shapes=scratch,
            compiler_params=pltpu.CompilerParams(collective_id=0, has_side_effects=True, vmem_limit_bytes=56 * 1024 * 1024),
        )(vel_u, vel_v, value_a11, salinity, surf_eta, trans_u, trans_v, bottom_depth, level_count, avg_weights, table)
        eta, tu, tv, gu, gv, cu, cv, cc, xu, xv, xt, xs = outs

        part = 16
        big = pl.BlockSpec((1, SLOT, part, L), lambda t, r: (t, 0, r, 0))
        small = pl.BlockSpec((1, part, L), lambda t, r: (t, r, 0))
        out = pl.BlockSpec((LEV, part, L), lambda t, r: (0, r, t))
        cube = jax.ShapeDtypeStruct((LEV, NR, NC), f32)
        u_new, v_new, t_new, s_new = pl.pallas_call(
            final_kernel,
            grid=(NT, NR // part),
            out_shape=[cube] * 4,
            in_specs=[smem] + [big] * 4 + [small] * 5,
            out_specs=[out] * 4,
        )(table, xu, xv, xt, xs, gu, gv, cu, cv, cc)
        return (eta, tu, tv, u_new, v_new, t_new, s_new)

    cube = P(None, 'row', 'col')
    flat = P('row', 'col')
    return jax.shard_map(step, mesh=mesh, in_specs=(cube, cube, cube, cube, flat, flat, flat, flat, flat, P()), out_specs=(flat, flat, flat, cube, cube, cube, cube), check_vma=False)
```

time: 1070 us -> 54.1 us (0.05); the launches traced: 1050 us -> 53.8 us
  other arithmetic: 535 us -> 0 us
  starting transfers between devices: 308 us -> 0 us
  waiting for transfers between devices: 153 us -> 0 us
  Pallas kernels: 0 us -> 51.2 us
  local copies, waits for them, and re-layouts: 51.3 us -> 1.9 us
    dynamic_update_slice x248 -> x0, other arithmetic: 397 us -> none  [tri_solve(): lax.scan(down, start, (low_links, up_links, right_side))]
    ppermute x143 -> x0, starting transfers between devices: 308 us -> none  [the longest x35 179 us: exchange(): from_south = lax.ppermute(wide[..., -1:, :], 'row', north_moves)]
    ppermute x143 -> x0, waiting for transfers between devices: 153 us -> none  [the longest x36 87.3 us: exchange(): from_west = lax.ppermute(field[..., -1:], 'col', east_moves)]
    add x62 -> x0, other arithmetic: 68.8 us -> none  [the longest x30 25 us: subcycle(): acc_u + weight * trans_u_new]
    pallas_call x0 -> x2, Pallas kernels: none -> 51.2 us  [the longest x1 41.4 us: step(): pl.pallas_call(functools.partial(ocean_kernel, tuple(mesh.axis_names), n_...]
    sub x32 -> x0, other arithmetic: 23 us -> none  [the longest x2 17.6 us: advect(): tracer_mid - 0.5 * TIME_STEP * (flux_east - flux_west + flux_north - flux...]
    another operation x12 -> x0, local copies, waits for them, and re-layouts: 18.6 us -> none
    dynamic_slice x30 -> x0, local copies, waits for them, and re-layouts: 17.7 us -> none  [step(): lax.scan(subcycle, (surf_eta, trans_u, trans_v, zero_field, zero_field),...]
  transfers between devices with their start and end apart: 143 -> 0, of which waited for: 95 -> 0; matrix products, arithmetic and copies ran while one was open for 49% -> 0% of each run, Pallas kernels for 0% -> 0%
where the time goes in v1:
time: 54.1 us; the launch traced here: 53.8 us
  Pallas kernels  51.2 us (95%)
  local copies, waits for them, and re-layouts  1.9 us (4%)
  between operations  0.68 us (1%)
    pallas_call x1, Pallas kernels, step(): pl.pallas_call(functools.partial(ocean_kernel, tuple(mesh.axis_names), n_...  41.4 us
    pallas_call x1, Pallas kernels, step(): pl.pallas_call(final_kernel, grid=(NT, NR // part), out_shape=[cube] * 4,...  9.83 us
    unnamed x9, local copies, waits for them, and re-layouts  1.9 us

profile of v1, /device:TPU:1, one launch (start us, length us, event | category | flops | bytes accessed | tf_op | source)
XLA Modules:
  0.0 53.8 jit_solution(8420385368701242867)
XLA Ops:
  0.6 41.4 %shard_map.162 = (f32[32,512]{1,0:T(8,128)}, f32[32,512]{1,0:T(8,128)}, f32[32,512]{1,0:T(8,128)}, f32[4,32,128]{2,1,0:T(8,128)}, f32[4,32,128]{2,1,0:T(8,128)},...) custom-call(f32[31,32,512]{2,1,0:T(8,128)} %refs_0_.1, ...), custom_call_target="tpu_custom_call" | custom-call | tf_op jit(solution)/shard_map/pallas_call | solution.py:510
  42.0 0.0 copy-start.2
  42.0 0.0 copy-start.1
  42.0 0.0 copy-start
  42.0 9.8 %shard_map.163 = (f32[31,32,512]{2,1,0:T(8,128)}, f32[31,32,512]{2,1,0:T(8,128)}, f32[31,32,512]{2,1,0:T(8,128)}, f32[31,32,512]{2,1,0:T(8,128)}) custom-call(f32[256]{0:T(256)} %constant.2.clone.refs_10_.tab_s, f32[4,32,32,128]{3,2,1,0:T(8,128)} %get-tuple-element.26.xu, f32[4,32,32,128]{3,2,1,0:T(8,128)} %get-tuple-element.27.xv, ...), custom_call_target="tpu_custom_call" | custom-call | tf_op jit(solution)/shard_map/pallas_call | solution.py:525
  51.9 0.0 copy-done.2
  51.9 0.6 %copy.21 = f32[32,512]{1,0:T(8,128)} copy(f32[32,512]{1,0:T(8,128)S(1)} %copy-done.2) | data formatting | bytes 131072
  52.5 0.0 copy-done.1
  52.5 0.6 %copy.22 = f32[32,512]{1,0:T(8,128)} copy(f32[32,512]{1,0:T(8,128)S(1)} %copy-done.1) | data formatting | bytes 131072
  53.1 0.0 copy-done
  53.1 0.6 %copy.23 = f32[32,512]{1,0:T(8,128)} copy(f32[32,512]{1,0:T(8,128)S(1)} %copy-done) | data formatting | bytes 131072
Async XLA Ops:
  42.0 9.9 %copy-start.2 = (f32[32,512]{1,0:T(8,128)S(1)}, f32[32,512]{1,0:T(8,128)}, u32[]{:S(2)}) copy-start(f32[32,512]{1,0:T(8,128)} %get-tuple-element.46) | copy-start | bytes 196612
  42.0 10.5 %copy-start.1 = (f32[32,512]{1,0:T(8,128)S(1)}, f32[32,512]{1,0:T(8,128)}, u32[]{:S(2)}) copy-start(f32[32,512]{1,0:T(8,128)} %get-tuple-element.47) | copy-start | bytes 196612
  42.0 11.1 %copy-start = (f32[32,512]{1,0:T(8,128)S(1)}, f32[32,512]{1,0:T(8,128)}, u32[]{:S(2)}) copy-start(f32[32,512]{1,0:T(8,128)} %get-tuple-element.48) | copy-start | bytes 196612

commit v2 on v1

--- a/solution.py
+++ b/solution.py
@@ -30,6 +30,7 @@
 XO = 40
 MESH = pl.DeviceIdType.MESH
 f32 = jnp.float32
+UNROLL = 4
 
 
 def solve_table(n_levels):
@@ -48,13 +49,13 @@
 
 
 def ocean_kernel(axes, n_col, n_row, n_sub, *refs):
-    (u_h, v_h, t_h, s_h, eta_h, tu_h, tv_h, dep_h, cnt_h, w_s, tab_s,
+    (u_h, v_h, t_h, s_h, eta_h, tu_h, tv_h, dep_h, cnt_h, w_h, tab_h,
      eta_o, tu_o, tv_o, gu_o, gv_o, cu_o, cv_o, cc_o, xu_o, xv_o, xt_o, xs_o,
      bu, bv, bt, bs, xu, xv, xt, xs, cnt_i, pc, pp, ce,
      pw, pe, rw, re, x, xf, qw, qe, we, ww, fw, fe, fre, frw,
      fu4, fv4, cu, cv, cvs, hu, hv, su, sv,
      ca, cb, cc, cd, cg, ch, cm, cn, tt, ss, au, av,
-     lsem, ssem, rsem, osem) = refs
+     w_s, tab_s, lsem, ssem, rsem, osem) = refs
     col = lax.axis_index('col')
     row = lax.axis_index('row')
     east = lax.rem(col + 1, n_col)
@@ -79,7 +80,10 @@
         flat_loads.append(pltpu.make_async_copy(dep_h.at[:, L * t:L * t + L], bv.at[t, LEV, R0:R0 + NR, :], lsem.at[len(loads) + len(flat_loads)]))
     for t in range(NT):
         flat_loads.append(pltpu.make_async_copy(cnt_h.at[:, L * t:L * t + L], cnt_i.at[t], lsem.at[len(loads) + len(flat_loads)]))
-    for cp in flat_loads + loads:
+    scalar_loads = [pltpu.make_async_copy(w_h, w_s, lsem.at[36]), pltpu.make_async_copy(tab_h, tab_s, lsem.at[37])]
+    edge_loads = [loads[NT * f + t] for f in range(4) for t in (0, NT - 1)]
+    mid_loads = [loads[NT * f + t] for f in range(4) for t in range(1, NT - 1)]
+    for cp in edge_loads + flat_loads + mid_loads + scalar_loads:
         cp.start()
 
     zero = functools.partial(jnp.zeros, dtype=f32)
@@ -216,7 +220,7 @@
     qw[...] = first
     qe[...] = last
 
-    for cp in loads:
+    for cp in edge_loads:
         cp.wait()
     first = last = zero((NR, L))
     for f, b in enumerate(bufs):
@@ -226,9 +230,13 @@
             last = jnp.where(lane == p, roll(b[NT - 1, k, R0:R0 + NR, :], (p + 1) % L), last)
     pw[...] = first
     pe[...] = last
+    for cp in mid_loads:
+        cp.wait()
     start(row_group)
     start(lane_group)
     start(wide_group)
+    for cp in scalar_loads:
+        cp.wait()
 
     row_pos = (row * NR + lax.broadcasted_iota(jnp.int32, (NR, L), 0)).astype(f32)
     total_rows = NR * n_row
@@ -270,13 +278,21 @@
         cv_o[t] = jnp.minimum(c_mid[t], c_north[t])
         cc_o[t] = c_mid[t]
 
+    def each_level(fn, unroll=UNROLL):
+        def some(i, _):
+            base = i * unroll
+            for j in range(unroll):
+                fn(base + j, base + j - 1 if j else jnp.maximum(base - 1, 0))
+            return 0
+
+        lax.fori_loop(0, SLOT // unroll, some, 0)
+
     for t in range(NT):
         pc[t] = zero((NR + 8, L))
     ce[...] = zero((NR, L))
     p_scale = BC_GRAVITY / LEV
 
-    def momentum_down(k, _):
-        prev = jnp.maximum(k - 1, 0)
+    def momentum_down(k, prev):
         scale, carry = tab_s[k], tab_s[SLOT + k]
         um, un, us = level(bu, k), level(bu, k, R0 + 1), level(bu, k, R0 - 1)
         vm, vn, vs = level(bv, k), level(bv, k, R0 + 1), level(bv, k, R0 - 1)
@@ -306,30 +322,29 @@
             v_star = vm[t] - ub4 * (fv4[...] + 0.125 * (ve[t] - vw[t])) - vm[t] * (0.5 * (vn[t] - vs[t])) + (pm[t] - pn)
             xu[t, k] = scale * u_star + carry * xu[t, prev]
             xv[t, k] = scale * v_star + carry * xv[t, prev]
-        return 0
-
-    lax.fori_loop(0, LEV, momentum_down, 0)
-
-    for t in range(NT):
-        def momentum_up(i, state, t=t):
-            k = LEV - 1 - i
+
+    each_level(momentum_down)
+
+    def momentum_up(t, _):
+        z = zero((NR, L))
+        state = [[z, z, z], [z, z, z]]
+        for k in range(LEV - 1, -1, -1):
             link, last_ = tab_s[2 * SLOT + k], tab_s[3 * SLOT + k]
-            kf = k.astype(f32)
-            out = []
-            for sweep, b, count, (below, sum_x, sum_0) in ((xu, bu, cu, state[:3]), (xv, bv, cv, state[3:])):
+            for q, (sweep, b, count) in enumerate(((xu, bu, cu), (xv, bv, cv))):
+                below, sum_x, sum_0 = state[q]
                 value = sweep[t, k]
-                active = count[t] > kf
-                solved = jnp.where(count[t] > kf + 1.0, value + link * below, jnp.where(active, last_ * value, 0.0))
+                active = count[t] > float(k)
+                solved = jnp.where(count[t] > float(k + 1), value + link * below, jnp.where(active, last_ * value, 0.0))
                 sweep[t, k] = solved
-                out += [solved, sum_x + solved, sum_0 + jnp.where(active, b[t, k, R0:R0 + NR, :], 0.0)]
-            return tuple(out)
-
-        z = zero((NR, L))
-        _, ux, u0, _, vx, v0 = lax.fori_loop(0, LEV, momentum_up, (z,) * 6)
-        for q, h, mean, count, total, start_ in ((0, hu, su, cu, ux, u0), (1, hv, sv, cv, vx, v0)):
+                state[q] = [solved, sum_x + solved, sum_0 + jnp.where(active, b[t, k, R0:R0 + NR, :], 0.0)]
+        for q, (h, mean, count) in enumerate(((hu, su, cu), (hv, sv, cv))):
+            _, total, start_ = state[q]
             n_active = jnp.maximum(count[t], 1.0)
             mean[t] = total / n_active
             xf[q, t, XO:XO + NR, :] = h[t] * (total - start_) / n_active / TIME_STEP
+        return 0
+
+    lax.fori_loop(0, NT, momentum_up, 0)
 
     stores = [pltpu.make_async_copy(a, o, osem.at[i]) for i, (a, o) in enumerate(((xu, xu_o), (xv, xv_o), (xt, xt_o), (xs, xs_o)))]
     first, last = pack_wide(xf, 2)
@@ -341,8 +356,7 @@
 
     c_west0 = jnp.minimum(west_lane(0, LEV), bu[0, LEV, R0:R0 + NR, :])
 
-    def tracer_down(k, _):
-        prev = jnp.maximum(k - 1, 0)
+    def tracer_down(k, prev):
         scale, carry = tab_s[4 * SLOT + k], tab_s[5 * SLOT + k]
         kf = k.astype(f32)
         um = [jnp.where(cu[t] > kf, bu[t, k, R0:R0 + NR, :], 0.0) for t in range(NT)]
@@ -359,9 +373,8 @@
                 f_south = vs[t] * (b[t, k, R0 - 1:R0 - 1 + NR, :] + q[t])
                 new = q[t] - 0.5 * TIME_STEP * (f_east[t] - f_west[t] + f_north - f_south)
                 sweep[t, k] = jnp.where(bu[t, LEV, R0:R0 + NR, :] > kf, scale * new + carry * sweep[t, prev], new)
-        return 0
-
-    lax.fori_loop(0, LEV, tracer_down, 0)
+
+    each_level(tracer_down)
     stores[2].start()
     stores[3].start()
 
@@ -465,23 +478,18 @@
     rows = u_o.shape[1]
     g_u, g_v, c_u, c_v, c_c = gu[0], gv[0], cu[0], cv[0], cc[0]
 
-    def up(i, state):
-        k = LEV - 1 - i
-        kf = k.astype(f32)
+    state = [jnp.zeros((rows, L), f32)] * 2
+    for k in range(LEV - 1, -1, -1):
+        kf = float(k)
         link, last = tab_s[6 * SLOT + k], tab_s[7 * SLOT + k]
         u_o[k] = jnp.where(c_u > kf, xu[0, k] + g_u, 0.0)
         v_o[k] = jnp.where(c_v > kf, xv[0, k] + g_v, 0.0)
         inner, active = c_c > kf + 1.0, c_c > kf
-        out = []
-        for sweep, o, below in ((xt, t_o, state[0]), (xs, s_o, state[1])):
+        for q, (sweep, o) in enumerate(((xt, t_o), (xs, s_o))):
             value = sweep[0, k]
-            solved = jnp.where(inner, value + link * below, jnp.where(active, last * value, value))
+            solved = jnp.where(inner, value + link * state[q], jnp.where(active, last * value, value))
             o[k] = solved
-            out.append(solved)
-        return tuple(out)
-
-    z = jnp.zeros((rows, L), f32)
-    lax.fori_loop(0, LEV, up, (z, z))
+            state[q] = solved
 
 
 def solution(mesh):
@@ -506,11 +514,12 @@
                    + [V((NR, L), f32)] * 2 + [V((3, NR, L), f32)] * 2
                    + [V((NR, L), f32)] * 2 + [V((NT, NR, L), f32)] * 7
                    + [V(wide, f32)] * 10 + [V((NT, NR, L), f32)] * 2
+                   + [pltpu.SMEM((n_sub,), f32), pltpu.SMEM((8 * SLOT,), f32)]
                    + [pltpu.SemaphoreType.DMA((40,)), pltpu.SemaphoreType.DMA((28,)), pltpu.SemaphoreType.DMA((28,)), pltpu.SemaphoreType.DMA((4,))])
         outs = pl.pallas_call(
             functools.partial(ocean_kernel, tuple(mesh.axis_names), n_col, n_row, n_sub),
             out_shape=[flat] * 3 + [tile] * 5 + [sweep] * 4,
-            in_specs=[hbm] * 9 + [smem] * 2,
+            in_specs=[hbm] * 11,
             out_specs=[vmem] * 8 + [hbm] * 4,
             scratch_shapes=scratch,
             compiler_params=pltpu.CompilerParams(collective_id=0, has_side_effects=True, vmem_limit_bytes=56 * 1024 * 1024),

time: 54.1 us -> 48.4 us (0.89)
  Pallas kernels: 51.2 us -> 45.5 us
    pallas_call x1, Pallas kernels: 41.4 us -> 36.2 us  [step(): pl.pallas_call(functools.partial(ocean_kernel, tuple(mesh.axis_names), n_...]
    pallas_call x1, Pallas kernels: 9.83 us -> 9.24 us  [step(): pl.pallas_call(final_kernel, grid=(NT, NR // part), out_shape=[cube] * 4,...]
where the time goes in v2:
time: 48.4 us; the launch traced here: 48 us
  Pallas kernels  45.5 us (94%)
  local copies, waits for them, and re-layouts  1.9 us (4%)
  between operations  0.68 us (1%)
    pallas_call x1, Pallas kernels, step(): pl.pallas_call(functools.partial(ocean_kernel, tuple(mesh.axis_names), n_...  36.2 us
    pallas_call x1, Pallas kernels, step(): pl.pallas_call(final_kernel, grid=(NT, NR // part), out_shape=[cube] * 4,...  9.24 us
    unnamed x9, local copies, waits for them, and re-layouts  1.9 us

profile of v2, /device:TPU:1, one launch (start us, length us, event | category | flops | bytes accessed | tf_op | source)
XLA Modules:
  0.0 48.0 jit_solution(10453664074783706747)
XLA Ops:
  0.6 36.2 %shard_map.162 = (f32[32,512]{1,0:T(8,128)}, f32[32,512]{1,0:T(8,128)}, f32[32,512]{1,0:T(8,128)}, f32[4,32,128]{2,1,0:T(8,128)}, f32[4,32,128]{2,1,0:T(8,128)},...) custom-call(f32[31,32,512]{2,1,0:T(8,128)} %refs_0_.1, ...), custom_call_target="tpu_custom_call" | custom-call | tf_op jit(solution)/shard_map/pallas_call | solution.py:519
  36.9 0.0 copy-start.2
  36.9 0.0 copy-start.1
  36.9 0.0 copy-start
  36.9 9.2 %shard_map.163 = (f32[31,32,512]{2,1,0:T(8,128)}, f32[31,32,512]{2,1,0:T(8,128)}, f32[31,32,512]{2,1,0:T(8,128)}, f32[31,32,512]{2,1,0:T(8,128)}) custom-call(f32[256]{0:T(256)} %constant.2.clone.refs_10_.tab_s, f32[4,32,32,128]{3,2,1,0:T(8,128)} %get-tuple-element.26.xu, f32[4,32,32,128]{3,2,1,0:T(8,128)} %get-tuple-element.27.xv, ...), custom_call_target="tpu_custom_call" | custom-call | tf_op jit(solution)/shard_map/pallas_call | solution.py:534
  46.1 0.0 copy-done.2
  46.2 0.6 %copy.21 = f32[32,512]{1,0:T(8,128)} copy(f32[32,512]{1,0:T(8,128)S(1)} %copy-done.2) | data formatting | bytes 131072
  46.8 0.0 copy-done.1
  46.8 0.6 %copy.22 = f32[32,512]{1,0:T(8,128)} copy(f32[32,512]{1,0:T(8,128)S(1)} %copy-done.1) | data formatting | bytes 131072
  47.4 0.0 copy-done
  47.4 0.6 %copy.23 = f32[32,512]{1,0:T(8,128)} copy(f32[32,512]{1,0:T(8,128)S(1)} %copy-done) | data formatting | bytes 131072
Async XLA Ops:
  36.9 9.3 %copy-start.2 = (f32[32,512]{1,0:T(8,128)S(1)}, f32[32,512]{1,0:T(8,128)}, u32[]{:S(2)}) copy-start(f32[32,512]{1,0:T(8,128)} %get-tuple-element.46) | copy-start | bytes 196612
  36.9 9.9 %copy-start.1 = (f32[32,512]{1,0:T(8,128)S(1)}, f32[32,512]{1,0:T(8,128)}, u32[]{:S(2)}) copy-start(f32[32,512]{1,0:T(8,128)} %get-tuple-element.47) | copy-start | bytes 196612
  36.9 10.5 %copy-start = (f32[32,512]{1,0:T(8,128)S(1)}, f32[32,512]{1,0:T(8,128)}, u32[]{:S(2)}) copy-start(f32[32,512]{1,0:T(8,128)} %get-tuple-element.48) | copy-start | bytes 196612

commit v3 on v2

--- a/solution.py
+++ b/solution.py
@@ -50,12 +50,12 @@
 
 def ocean_kernel(axes, n_col, n_row, n_sub, *refs):
     (u_h, v_h, t_h, s_h, eta_h, tu_h, tv_h, dep_h, cnt_h, w_h, tab_h,
-     eta_o, tu_o, tv_o, gu_o, gv_o, cu_o, cv_o, cc_o, xu_o, xv_o, xt_o, xs_o,
-     bu, bv, bt, bs, xu, xv, xt, xs, cnt_i, pc, pp, ce,
+     eta_o, tu_o, tv_o, gu_o, gv_o, cu, cv, cc_o, xu, xv, xt, xs,
+     bu, bv, bt, bs, bp, cnt_i, rp,
      pw, pe, rw, re, x, xf, qw, qe, we, ww, fw, fe, fre, frw,
-     fu4, fv4, cu, cv, cvs, hu, hv, su, sv,
-     ca, cb, cc, cd, cg, ch, cm, cn, tt, ss, au, av,
-     w_s, tab_s, lsem, ssem, rsem, osem) = refs
+     fu4, fv4, hu, hv, su, sv,
+     ca, cb, cc, cd, cg, ch, cm, cn, tt, au, av,
+     w_s, tab_s, lsem, ssem, rsem) = refs
     col = lax.axis_index('col')
     row = lax.axis_index('row')
     east = lax.rem(col + 1, n_col)
@@ -68,6 +68,26 @@
         return tuple(at[name] for name in axes)
 
     bufs = (bu, bv, bt, bs)
+    barrier = pltpu.get_barrier_semaphore()
+
+    def signal(c, r):
+        pl.semaphore_signal(barrier, inc=1, device_id=dev(c, r), device_id_type=MESH)
+
+    signal(west, row)
+    signal(east, row)
+
+    @pl.when(has_s)
+    def _():
+        for c in (west, col, east):
+            signal(c, row - 1)
+
+    @pl.when(has_n)
+    def _():
+        for c in (west, col, east):
+            signal(c, row + 1)
+
+    zero = functools.partial(jnp.zeros, dtype=f32)
+
     loads = []
     for f, (src, dst) in enumerate(zip((u_h, v_h, t_h, s_h), bufs)):
         for t in range(NT):
@@ -85,67 +105,6 @@
     mid_loads = [loads[NT * f + t] for f in range(4) for t in range(1, NT - 1)]
     for cp in edge_loads + flat_loads + mid_loads + scalar_loads:
         cp.start()
-
-    zero = functools.partial(jnp.zeros, dtype=f32)
-    for f in range(4):
-        for t in range(NT + 1):
-            x[f, t, 0:8, :] = zero((8, L))
-            x[f, t, XR - 8:XR, :] = zero((8, L))
-    for t in range(NT + 1):
-        tt[t, XR - 8:XR, :] = zero((8, L))
-    for t in range(NT):
-        bt[t, LEV, R0:R0 + NR, :] = zero((NR, L))
-        bs[t, LEV, R0:R0 + NR, :] = zero((NR, L))
-        for a in (xu, xv, xt, xs):
-            a[t, 0] = zero((NR, L))
-
-    @pl.when(jnp.logical_not(has_s))
-    def _():
-        for b in bufs:
-            b[:, :, R0 - 8:R0, :] = zero((NT, SLOT, 8, L))
-        re[R0 - 8:R0, :] = zero((8, L))
-        x[:, 0:NT, 8:XO, :] = zero((4, NT, NR, L))
-        xf[:, 0:NT, 8:XO, :] = zero((2, NT, NR, L))
-        for a in (we, ww, fre, frw):
-            a[0] = zero((NR, L))
-
-    @pl.when(jnp.logical_not(has_n))
-    def _():
-        for b in bufs:
-            b[:, :, R0 + NR:PR, :] = zero((NT, SLOT, 8, L))
-        rw[R0 + NR:PR, :] = zero((8, L))
-        x[:, 0:NT, XO + NR:XO + 2 * NR, :] = zero((4, NT, NR, L))
-        xf[:, 0:NT, XO + NR:XO + 2 * NR, :] = zero((2, NT, NR, L))
-        for a in (we, ww, fre, frw):
-            a[2] = zero((NR, L))
-
-    barrier = pltpu.get_barrier_semaphore()
-
-    def signal(c, r):
-        pl.semaphore_signal(barrier, inc=1, device_id=dev(c, r), device_id_type=MESH)
-
-    signal(west, row)
-    signal(east, row)
-
-    @pl.when(has_s)
-    def _():
-        for c in (west, col, east):
-            signal(c, row - 1)
-
-    @pl.when(has_n)
-    def _():
-        for c in (west, col, east):
-            signal(c, row + 1)
-
-    edge = jnp.logical_or(row == 0, row == n_row - 1)
-
-    @pl.when(edge)
-    def _():
-        pl.semaphore_wait(barrier, 5)
-
-    @pl.when(jnp.logical_not(edge))
-    def _():
-        pl.semaphore_wait(barrier, 8)
 
     n_copies = 0
 
@@ -198,6 +157,9 @@
 
     lane = lax.broadcasted_iota(jnp.int32, (NR, L), 1)
 
+    for t in range(NT):
+        bt[t, LEV, R0:R0 + NR, :] = zero((NR, L))
+        bs[t, LEV, R0:R0 + NR, :] = zero((NR, L))
     for cp in flat_loads:
         cp.wait()
     for t in range(NT):
@@ -232,51 +194,76 @@
     pe[...] = last
     for cp in mid_loads:
         cp.wait()
+    edge = jnp.logical_or(row == 0, row == n_row - 1)
+
+    @pl.when(edge)
+    def _():
+        pl.semaphore_wait(barrier, 5)
+
+    @pl.when(jnp.logical_not(edge))
+    def _():
+        pl.semaphore_wait(barrier, 8)
+
     start(row_group)
     start(lane_group)
     start(wide_group)
     for cp in scalar_loads:
         cp.wait()
 
+    for f in range(4):
+        for t in range(NT + 1):
+            x[f, t, 0:8, :] = zero((8, L))
+            x[f, t, XR - 8:XR, :] = zero((8, L))
+    for t in range(NT + 1):
+        tt[t, XR - 8:XR, :] = zero((8, L))
+    for t in range(NT):
+        for a in (xu, xv, xt, xs):
+            a[t, 0] = zero((NR, L))
+
+    @pl.when(jnp.logical_not(has_s))
+    def _():
+        for b in bufs:
+            b[:, :, R0 - 8:R0, :] = zero((NT, SLOT, 8, L))
+        re[R0 - 8:R0, :] = zero((8, L))
+        x[:, 0:NT, 8:XO, :] = zero((4, NT, NR, L))
+        xf[:, 0:NT, 8:XO, :] = zero((2, NT, NR, L))
+        for a in (we, ww, fre, frw):
+            a[0] = zero((NR, L))
+
+    @pl.when(jnp.logical_not(has_n))
+    def _():
+        for b in bufs:
+            b[:, :, R0 + NR:PR, :] = zero((NT, SLOT, 8, L))
+        rw[R0 + NR:PR, :] = zero((8, L))
+        x[:, 0:NT, XO + NR:XO + 2 * NR, :] = zero((4, NT, NR, L))
+        xf[:, 0:NT, XO + NR:XO + 2 * NR, :] = zero((2, NT, NR, L))
+        for a in (we, ww, fre, frw):
+            a[2] = zero((NR, L))
+
+
     row_pos = (row * NR + lax.broadcasted_iota(jnp.int32, (NR, L), 0)).astype(f32)
     total_rows = NR * n_row
     fu4[...] = 0.25 * (CORIO_F0 + CORIO_BETA * ((row_pos + 0.5) / total_rows - 0.5))
     fv4[...] = 0.25 * (CORIO_F0 + CORIO_BETA * ((row_pos + 1.0) / total_rows - 0.5))
 
     def to_east(tiles, halo):
+        last_lane = lane[:halo.shape[0]] == L - 1
         rolled = [roll(a, L - 1) for a in tiles] + [halo]
-        return [jnp.where(lane == L - 1, rolled[t + 1], rolled[t]) for t in range(NT)]
+        return [jnp.where(last_lane, rolled[t + 1], rolled[t]) for t in range(NT)]
 
     def to_west(tiles, halo):
+        first_lane = lane[:halo.shape[0]] == 0
         rolled = [halo] + [roll(a, 1) for a in tiles]
-        return [jnp.where(lane == 0, rolled[t], rolled[t + 1]) for t in range(NT)]
-
-    def east_lane(f, k, lo=R0):
-        return pltpu.roll(re[lo:lo + NR, :], L - 1 - (SLOT * f + k), 1)
-
-    def west_lane(f, k, lo=R0):
-        return pltpu.roll(rw[lo:lo + NR, :], lax.rem(L - (SLOT * f + k), L), 1)
-
-    arrive(row_group)
-    arrive(lane_group)
-
-    def level(b, k, lo=R0):
-        return [b[t, k, lo:lo + NR, :] for t in range(NT)]
-
-    c_mid, d_mid = level(bu, LEV), level(bv, LEV)
-    c_east = to_east(c_mid, east_lane(0, LEV))
-    d_east = to_east(d_mid, east_lane(1, LEV))
-    c_north, c_south = level(bu, LEV, R0 + 1), level(bu, LEV, R0 - 1)
-    d_north = level(bv, LEV, R0 + 1)
-    for t in range(NT):
-        cu[t] = jnp.minimum(c_mid[t], c_east[t])
-        cv[t] = jnp.minimum(c_mid[t], c_north[t])
-        cvs[t] = jnp.minimum(c_mid[t], c_south[t])
-        hu[t] = 0.5 * (d_mid[t] + d_east[t])
-        hv[t] = 0.5 * (d_mid[t] + d_north[t])
-        cu_o[t] = jnp.minimum(c_mid[t], c_east[t])
-        cv_o[t] = jnp.minimum(c_mid[t], c_north[t])
-        cc_o[t] = c_mid[t]
+        return [jnp.where(first_lane, rolled[t], rolled[t + 1]) for t in range(NT)]
+
+    def east_lane(f, k, lo=R0, n=NR):
+        return pltpu.roll(re[lo:lo + n, :], L - 1 - (SLOT * f + k), 1)
+
+    def west_lane(f, k, lo=R0, n=NR):
+        return pltpu.roll(rw[lo:lo + n, :], lax.rem(L - (SLOT * f + k), L), 1)
+
+    def level(b, k, lo=R0, n=NR):
+        return [b[t, k, lo:lo + n, :] for t in range(NT)]
 
     def each_level(fn, unroll=UNROLL):
         def some(i, _):
@@ -287,43 +274,73 @@
 
         lax.fori_loop(0, SLOT // unroll, some, 0)
 
-    for t in range(NT):
-        pc[t] = zero((NR + 8, L))
-    ce[...] = zero((NR, L))
     p_scale = BC_GRAVITY / LEV
 
-    def momentum_down(k, prev):
+    def pressure(t, lo, n):
+        total = zero((n, L))
+        for k in range(LEV):
+            density = CONTRACT_S * bs[t, k, lo:lo + n, :] - EXPAND_T * bt[t, k, lo:lo + n, :]
+            total = total + density
+            bp[t, k, lo:lo + n, :] = p_scale * (total - 0.5 * density)
+        bp[t, LEV, lo:lo + n, :] = zero((n, L))
+
+    def own_pressure(t, _):
+        pressure(t, R0, NR)
+        return 0
+
+    lax.fori_loop(0, NT, own_pressure, 0)
+
+    def momentum_down(parts, k, prev):
         scale, carry = tab_s[k], tab_s[SLOT + k]
-        um, un, us = level(bu, k), level(bu, k, R0 + 1), level(bu, k, R0 - 1)
-        vm, vn, vs = level(bv, k), level(bv, k, R0 + 1), level(bv, k, R0 - 1)
-        ue = to_east(um, east_lane(0, k))
-        uw = to_west(um, west_lane(0, k))
-        unw = to_west(un, west_lane(0, k, R0 + 1))
-        ve = to_east(vm, east_lane(1, k))
-        vw = to_west(vm, west_lane(1, k))
-        vse = to_east(vs, east_lane(1, k, R0 - 1))
-        pm = []
-        for t in range(NT):
-            density = CONTRACT_S * bs[t, k, R0:PR, :] - EXPAND_T * bt[t, k, R0:PR, :]
-            total = pc[t] + density
-            pc[t] = total
-            pressure = p_scale * (total - 0.5 * density)
-            pp[t] = pressure
-            pm.append(pressure[:NR])
-        density = CONTRACT_S * east_lane(3, k) - EXPAND_T * east_lane(2, k)
-        total = ce[...] + density
-        ce[...] = total
-        pe_ = to_east(pm, p_scale * (total - 0.5 * density))
-        for t in range(NT):
-            pn = pp[t, 1:NR + 1, :]
-            vb4 = (vm[t] + ve[t]) + (vs[t] + vse[t])
-            ub4 = (um[t] + uw[t]) + (un[t] + unw[t])
-            u_star = um[t] + vb4 * (fu4[...] - 0.125 * (un[t] - us[t])) - um[t] * (0.5 * (ue[t] - uw[t])) + (pm[t] - pe_[t])
-            v_star = vm[t] - ub4 * (fv4[...] + 0.125 * (ve[t] - vw[t])) - vm[t] * (0.5 * (vn[t] - vs[t])) + (pm[t] - pn)
-            xu[t, k] = scale * u_star + carry * xu[t, prev]
-            xv[t, k] = scale * v_star + carry * xv[t, prev]
-
-    each_level(momentum_down)
+        for lo, n in parts:
+            own = slice(lo - R0, lo - R0 + n)
+            um, un, us = level(bu, k, lo, n), level(bu, k, lo + 1, n), level(bu, k, lo - 1, n)
+            ue = to_east(um, east_lane(0, k, lo, n))
+            uw = to_west(um, west_lane(0, k, lo, n))
+            unw = to_west(un, west_lane(0, k, lo + 1, n))
+            vm, vn, vs = level(bv, k, lo, n), level(bv, k, lo + 1, n), level(bv, k, lo - 1, n)
+            ve = to_east(vm, east_lane(1, k, lo, n))
+            vw = to_west(vm, west_lane(1, k, lo, n))
+            vse = to_east(vs, east_lane(1, k, lo - 1, n))
+            pm, pn = level(bp, k, lo, n), level(bp, k, lo + 1, n)
+            pe_ = to_east(pm, pltpu.roll(rp[own, :], L - 1 - k, 1))
+            for t in range(NT):
+                vb4 = (vm[t] + ve[t]) + (vs[t] + vse[t])
+                ub4 = (um[t] + uw[t]) + (un[t] + unw[t])
+                u_star = um[t] + vb4 * (fu4[own, :] - 0.125 * (un[t] - us[t])) - um[t] * (0.5 * (ue[t] - uw[t])) + (pm[t] - pe_[t])
+                v_star = vm[t] - ub4 * (fv4[own, :] + 0.125 * (ve[t] - vw[t])) - vm[t] * (0.5 * (vn[t] - vs[t])) + (pm[t] - pn[t])
+                xu[t, k, own, :] = scale * u_star + carry * xu[t, prev, own, :]
+                xv[t, k, own, :] = scale * v_star + carry * xv[t, prev, own, :]
+
+    arrive(lane_group)
+    density = CONTRACT_S * roll(re[R0:R0 + NR, :], L - 3 * SLOT) - EXPAND_T * roll(re[R0:R0 + NR, :], L - 2 * SLOT)
+    total = density
+    for step in (1, 2, 4, 8, 16):
+        total = total + jnp.where(lane >= step, roll(total, step), 0.0)
+    rp[...] = p_scale * (total - 0.5 * density)
+    each_level(functools.partial(momentum_down, ((R0 + 8, NR - 16),)))
+    arrive(row_group)
+
+    def north_pressure(t, _):
+        pressure(t, R0 + NR, 8)
+        return 0
+
+    lax.fori_loop(0, NT, north_pressure, 0)
+    each_level(functools.partial(momentum_down, ((R0, 8), (R0 + NR - 8, 8))))
+    drain(row_group)
+
+    c_mid, d_mid = level(bu, LEV), level(bv, LEV)
+    c_east = to_east(c_mid, east_lane(0, LEV))
+    d_east = to_east(d_mid, east_lane(1, LEV))
+    c_north, c_south = level(bu, LEV, R0 + 1), level(bu, LEV, R0 - 1)
+    d_north = level(bv, LEV, R0 + 1)
+    for t in range(NT):
+        cu[t] = jnp.minimum(c_mid[t], c_east[t])
+        cv[t] = jnp.minimum(c_mid[t], c_north[t])
+        hu[t] = 0.5 * (d_mid[t] + d_east[t])
+        hv[t] = 0.5 * (d_mid[t] + d_north[t])
+        cc_o[t] = c_mid[t]
+    c_west0 = jnp.minimum(west_lane(0, LEV), c_mid[0])
 
     def momentum_up(t, _):
         z = zero((NR, L))
@@ -336,32 +353,30 @@
                 active = count[t] > float(k)
                 solved = jnp.where(count[t] > float(k + 1), value + link * below, jnp.where(active, last_ * value, 0.0))
                 sweep[t, k] = solved
-                state[q] = [solved, sum_x + solved, sum_0 + jnp.where(active, b[t, k, R0:R0 + NR, :], 0.0)]
+                start_ = jnp.where(active, b[t, k, R0:R0 + NR, :], 0.0)
+                b[t, k, R0:R0 + NR, :] = start_
+                state[q] = [solved, sum_x + solved, sum_0 + start_]
         for q, (h, mean, count) in enumerate(((hu, su, cu), (hv, sv, cv))):
             _, total, start_ = state[q]
             n_active = jnp.maximum(count[t], 1.0)
             mean[t] = total / n_active
             xf[q, t, XO:XO + NR, :] = h[t] * (total - start_) / n_active / TIME_STEP
+        c_south = jnp.minimum(bu[t, LEV, 0:8, :], pltpu.roll(bu[t, LEV, R0:R0 + 8, :], 7, 0))
+        for k in range(LEV):
+            bv[t, k, 0:8, :] = jnp.where(c_south > float(k), bv[t, k, 0:8, :], 0.0)
         return 0
 
     lax.fori_loop(0, NT, momentum_up, 0)
 
-    stores = [pltpu.make_async_copy(a, o, osem.at[i]) for i, (a, o) in enumerate(((xu, xu_o), (xv, xv_o), (xt, xt_o), (xs, xs_o)))]
     first, last = pack_wide(xf, 2)
     fw[...] = first
     fe[...] = last
     start(force_group)
-    stores[0].start()
-    stores[1].start()
-
-    c_west0 = jnp.minimum(west_lane(0, LEV), bu[0, LEV, R0:R0 + NR, :])
 
     def tracer_down(k, prev):
         scale, carry = tab_s[4 * SLOT + k], tab_s[5 * SLOT + k]
-        kf = k.astype(f32)
-        um = [jnp.where(cu[t] > kf, bu[t, k, R0:R0 + NR, :], 0.0) for t in range(NT)]
-        vm = [jnp.where(cv[t] > kf, bv[t, k, R0:R0 + NR, :], 0.0) for t in range(NT)]
-        vs = [jnp.where(cvs[t] > kf, bv[t, k, R0 - 1:R0 - 1 + NR, :], 0.0) for t in range(NT)]
+        kf = lax.convert_element_type(k, f32)
+        um, vm, vs = level(bu, k), level(bv, k), level(bv, k, R0 - 1)
         uw0 = jnp.where(c_west0 > kf, west_lane(0, k), 0.0)
         for f, b, sweep in ((2, bt, xt), (3, bs, xs)):
             q = level(b, k)
@@ -375,8 +390,6 @@
                 sweep[t, k] = jnp.where(bu[t, LEV, R0:R0 + NR, :] > kf, scale * new + carry * sweep[t, prev], new)
 
     each_level(tracer_down)
-    stores[2].start()
-    stores[3].start()
 
     arrive(wide_group)
     drain(wide_group)
@@ -424,7 +437,7 @@
         au[t] = zero((NR, L))
         av[t] = zero((NR, L))
 
-    def subcycle(lo, hi, chunk, n, _):
+    def subcycle(lo, hi, chunk, masked, n, _):
         lane_c = lax.broadcasted_iota(jnp.int32, (chunk, L), 1)
         first_lane, last_lane = lane_c == 0, lane_c == L - 1
         weight = w_s[n]
@@ -435,18 +448,20 @@
                 v_t, v_s = x[2, t, r:r + chunk, :], x[2, t, r - 1:r - 1 + chunk, :]
                 x[0, t, r:r + chunk, :] = x[0, t, r:r + chunk, :] - dt_fast * ((u_t[t] - u_w[t]) + (v_t - v_s))
                 tt[t, r:r + chunk, :] = u_t[t] + u_w[t]
-                ss[t, r:r + chunk, :] = v_t + v_s
-        for r in range(lo, hi, chunk):
+        for r in range(hi - chunk, lo - 1, -chunk):
             e_t = [x[0, t, r:r + chunk, :] for t in range(XT)]
             e_e = ring_east(e_t, last_lane)
-            s_t = [ss[t, r:r + chunk, :] for t in range(XT)]
+            v_t = [x[2, t, r:r + chunk, :] for t in range(XT)]
+            s_t = [v_t[t] + x[2, t, r - 1:r - 1 + chunk, :] for t in range(XT)]
             s_e = ring_east(s_t, last_lane)
             for t in range(XT):
                 at = (t, slice(r, r + chunk))
                 up = (t, slice(r + 1, r + 1 + chunk))
                 e_n = x[0, t, r + 1:r + 1 + chunk, :]
-                x[1, t, r:r + chunk, :] = cm[at] * x[1, t, r:r + chunk, :] + ca[at] * (s_t[t] + s_e[t]) + cc[at] - cb[at] * (e_e[t] - e_t[t])
-                x[2, t, r:r + chunk, :] = cn[at] * x[2, t, r:r + chunk, :] - cd[at] * (tt[at] + tt[up]) + ch[at] - cg[at] * (e_n - e_t[t])
+                u_old = x[1, t, r:r + chunk, :] if masked else cm[at] * x[1, t, r:r + chunk, :]
+                v_old = v_t[t] if masked else cn[at] * v_t[t]
+                x[1, t, r:r + chunk, :] = u_old + ca[at] * (s_t[t] + s_e[t]) + cc[at] - cb[at] * (e_e[t] - e_t[t])
+                x[2, t, r:r + chunk, :] = v_old - cd[at] * (tt[at] + tt[up]) + ch[at] - cg[at] * (e_n - e_t[t])
         for t in range(NT):
             au[t] += weight * x[1, t, XO:XO + NR, :]
             av[t] += weight * x[2, t, XO:XO + NR, :]
@@ -457,25 +472,27 @@
         until = n_sub - 8 * (side - 1)
         rows = NR + 16 * side
         chunk = {4: 32, 3: 40, 2: 32, 1: 24}[side]
-        lax.fori_loop(done, until, functools.partial(subcycle, XO - 8 * side, XO - 8 * side + rows, chunk), 0)
+        stretch = functools.partial(subcycle, XO - 8 * side, XO - 8 * side + rows, chunk)
+        if done == 0:
+            stretch(False, 0, 0)
+            done = 1
+        lax.fori_loop(done, until, functools.partial(stretch, True), 0)
         done = until
 
     for t in range(NT):
-        cols = slice(L * t, L * t + L)
-        eta_o[:, cols] = x[0, t, XO:XO + NR, :]
-        tu_o[:, cols] = x[1, t, XO:XO + NR, :]
-        tv_o[:, cols] = x[2, t, XO:XO + NR, :]
+        eta_o[t] = x[0, t, XO:XO + NR, :]
+        tu_o[t] = x[1, t, XO:XO + NR, :]
+        tv_o[t] = x[2, t, XO:XO + NR, :]
         gu_o[t] = au[t] / hu[t] - su[t]
         gv_o[t] = av[t] / hv[t] - sv[t]
 
-    for group in (row_group, lane_group, force_group):
+    for group in (lane_group, force_group):
         drain(group)
-    for cp in stores:
-        cp.wait()
-
-
-def final_kernel(tab_s, xu, xv, xt, xs, gu, gv, cu, cv, cc, u_o, v_o, t_o, s_o):
+
+
+def final_kernel(tab_s, xu, xv, xt, xs, gu, gv, cu, cv, cc, eta, tu, tv, eta_o, tu_o, tv_o, u_o, v_o, t_o, s_o):
     rows = u_o.shape[1]
+    eta_o[...], tu_o[...], tv_o[...] = eta[0], tu[0], tv[0]
     g_u, g_v, c_u, c_v, c_c = gu[0], gv[0], cu[0], cv[0], cc[0]
 
     state = [jnp.zeros((rows, L), f32)] * 2
@@ -499,46 +516,46 @@
     def step(vel_u, vel_v, value_a11, salinity, surf_eta, trans_u, trans_v, bottom_depth, level_count, avg_weights):
         n_sub = avg_weights.shape[0]
         table = jnp.asarray(solve_table(LEV))
-        hbm = pl.BlockSpec(memory_space=pl.ANY)
+        hbm = pl.BlockSpec(memory_space=pltpu.HBM)
         vmem = pl.BlockSpec(memory_space=pltpu.VMEM)
         smem = pl.BlockSpec(memory_space=pltpu.SMEM)
-        flat = jax.ShapeDtypeStruct((NR, NC), f32)
-        tile = jax.ShapeDtypeStruct((NT, NR, L), f32)
-        sweep = jax.ShapeDtypeStruct((NT, SLOT, NR, L), f32)
         V = pltpu.VMEM
+        tile = V((NT, NR, L), f32)
+        sweep = V((NT, SLOT, NR, L), f32)
         wide = (NT + 1, XR, L)
-        scratch = ([V((NT, SLOT, PR, L), f32)] * 4 + [V((NT, SLOT, NR, L), f32)] * 4
-                   + [V((NT, NR, L), jnp.int32), V((NT, NR + 8, L), f32), V((NT, NR + 8, L), f32), V((NR, L), f32)]
+        scratch = ([V((NT, SLOT, PR, L), f32)] * 5 + [V((NT, NR, L), jnp.int32), V((NR, L), f32)]
                    + [V((NR, L), f32)] * 2 + [V((PR, L), f32)] * 2
                    + [V((4,) + wide, f32), V((2,) + wide, f32)] + [V((NR, L), f32)] * 2 + [V((3, NR, L), f32)] * 2
                    + [V((NR, L), f32)] * 2 + [V((3, NR, L), f32)] * 2
-                   + [V((NR, L), f32)] * 2 + [V((NT, NR, L), f32)] * 7
-                   + [V(wide, f32)] * 10 + [V((NT, NR, L), f32)] * 2
+                   + [V((NR, L), f32)] * 2 + [V((NT, NR, L), f32)] * 4
+                   + [V(wide, f32)] * 9 + [V((NT, NR, L), f32)] * 2
                    + [pltpu.SMEM((n_sub,), f32), pltpu.SMEM((8 * SLOT,), f32)]
-                   + [pltpu.SemaphoreType.DMA((40,)), pltpu.SemaphoreType.DMA((28,)), pltpu.SemaphoreType.DMA((28,)), pltpu.SemaphoreType.DMA((4,))])
+                   + [pltpu.SemaphoreType.DMA((40,)), pltpu.SemaphoreType.DMA((28,)), pltpu.SemaphoreType.DMA((28,))])
         outs = pl.pallas_call(
             functools.partial(ocean_kernel, tuple(mesh.axis_names), n_col, n_row, n_sub),
-            out_shape=[flat] * 3 + [tile] * 5 + [sweep] * 4,
+            out_shape=[tile] * 8 + [sweep] * 4,
             in_specs=[hbm] * 11,
-            out_specs=[vmem] * 8 + [hbm] * 4,
+            out_specs=[vmem] * 12,
             scratch_shapes=scratch,
-            compiler_params=pltpu.CompilerParams(collective_id=0, has_side_effects=True, vmem_limit_bytes=56 * 1024 * 1024),
-        )(vel_u, vel_v, value_a11, salinity, surf_eta, trans_u, trans_v, bottom_depth, level_count, avg_weights, table)
-        eta, tu, tv, gu, gv, cu, cv, cc, xu, xv, xt, xs = outs
+            compiler_params=pltpu.CompilerParams(collective_id=0, has_side_effects=True, vmem_limit_bytes=32 * 1024 * 1024),
+        )(*[pltpu.with_memory_space_constraint(a, pltpu.HBM) for a in (vel_u, vel_v, value_a11, salinity, surf_eta, trans_u, trans_v, bottom_depth, level_count, avg_weights, table)])
+        eta, tu, tv, gu, gv, cu, cv, cc, xu, xv, xt, xs = [pltpu.with_memory_space_constraint(o, pltpu.VMEM) for o in outs]
 
         part = 16
         big = pl.BlockSpec((1, SLOT, part, L), lambda t, r: (t, 0, r, 0))
         small = pl.BlockSpec((1, part, L), lambda t, r: (t, r, 0))
         out = pl.BlockSpec((LEV, part, L), lambda t, r: (0, r, t))
+        out_flat = pl.BlockSpec((part, L), lambda t, r: (r, t))
         cube = jax.ShapeDtypeStruct((LEV, NR, NC), f32)
-        u_new, v_new, t_new, s_new = pl.pallas_call(
+        flat = jax.ShapeDtypeStruct((NR, NC), f32)
+        return tuple(pl.pallas_call(
             final_kernel,
             grid=(NT, NR // part),
-            out_shape=[cube] * 4,
-            in_specs=[smem] + [big] * 4 + [small] * 5,
-            out_specs=[out] * 4,
-        )(table, xu, xv, xt, xs, gu, gv, cu, cv, cc)
-        return (eta, tu, tv, u_new, v_new, t_new, s_new)
+            out_shape=[flat] * 3 + [cube] * 4,
+            in_specs=[smem] + [big] * 4 + [small] * 8,
+            out_specs=[out_flat] * 3 + [out] * 4,
+            compiler_params=pltpu.CompilerParams(vmem_limit_bytes=24 * 1024 * 1024),
+        )(table, xu, xv, xt, xs, gu, gv, cu, cv, cc, eta, tu, tv))
 
     cube = P(None, 'row', 'col')
     flat = P('row', 'col')

time: 48.4 us -> 43.2 us (0.89)
  Pallas kernels: 45.5 us -> 42.4 us
  local copies, waits for them, and re-layouts: 1.9 us -> 0.01 us
    pallas_call x1, Pallas kernels: 9.24 us -> 5.68 us  [step(): pl.pallas_call(final_kernel, grid=(NT, NR // part), out_shape=[flat] * 3...]
    unnamed x9 -> x2, local copies, waits for them, and re-layouts: 1.9 us -> 0.01 us
    pallas_call x1, Pallas kernels: 36.2 us -> 36.8 us  [step(): pl.pallas_call(functools.partial(ocean_kernel, tuple(mesh.axis_names), n_...]
where the time goes in v3:
time: 43.2 us; the launch traced here: 43.1 us
  Pallas kernels  42.4 us (98%)
  between operations  0.66 us (2%)
    pallas_call x1, Pallas kernels, step(): pl.pallas_call(functools.partial(ocean_kernel, tuple(mesh.axis_names), n_...  36.8 us
    pallas_call x1, Pallas kernels, step(): pl.pallas_call(final_kernel, grid=(NT, NR // part), out_shape=[flat] * 3...  5.68 us

profile of v3, /device:TPU:1, one launch (start us, length us, event | category | flops | bytes accessed | tf_op | source)
XLA Modules:
  0.0 43.1 jit_solution(15501991259139742526)
XLA Ops:
  0.6 0.0 copy-start
  0.6 36.8 %shard_map.162 = (f32[4,32,128]{2,1,0:T(8,128)S(1)}, f32[4,32,128]{2,1,0:T(8,128)S(1)}, f32[4,32,128]{2,1,0:T(8,128)S(1)}, f32[4,32,128]{2,1,0:T(8,128)S(1)}, f3...) custom-call(f32[31,32,512]{2,1,0:T(8,128)} %refs_0_.1, ...), custom_call_target="tpu_custom_call" | custom-call | tf_op jit(solution)/shard_map/pallas_call | solution.py:534
  37.4 0.0 copy-done
  37.4 5.7 %shard_map.163 = (f32[32,512]{1,0:T(8,128)}, f32[32,512]{1,0:T(8,128)}, f32[32,512]{1,0:T(8,128)}, f32[31,32,512]{2,1,0:T(8,128)}, f32[31,32,512]{2,1,0:T(8,128)...) custom-call(f32[256]{0:T(256)S(1)} %copy-done, f32[4,32,32,128]{3,2,1,0:T(8,128)S(1)} %get-tuple-element.19.xu, ...), custom_call_target="tpu_custom_call" | custom-call | tf_op jit(solution)/shard_map/pallas_call | solution.py:551
Async XLA Ops:
  0.6 36.8 %copy-start = (f32[256]{0:T(256)S(1)}, f32[256]{0:T(256)}, u32[]{:S(2)}) copy-start(f32[256]{0:T(256)} %constant.2.clone.refs_10_.tab_s) | copy-start | bytes 3076
